TPU v7x, 8 devices: a whole 2x2x1 slice. The times are simulated.
8 devices in a mesh: outer: 2 (over z, y), middle: 2 (over x), inner: 2 (over core).
Axes of the slice: x: 2, y: 2, z: 1, core: 2. Of those that a mesh axis runs over, the one named last changes fastest.
Arguments:
- g_embed: float32 [8, 32768, 128], P(('outer', 'middle', 'inner'))
- g_attn: float32 [8, 16, 128, 512], P(('outer', 'middle', 'inner'))
- g_ffn_in: float32 [8, 16, 128, 512], P(('outer', 'middle', 'inner'))
- g_ffn_out: float32 [8, 16, 512, 128], P(('outer', 'middle', 'inner'))
- g_vec: float32 [8, 16, 1664], P(('outer', 'middle', 'inner'))
- m_flat: float32 [7366656], P(('outer', 'middle', 'inner'))
- v_flat: float32 [7366656], P(('outer', 'middle', 'inner'))
- w_flat: float32 [7366656], P(('outer', 'middle', 'inner'))
Outputs:
- output 1: float32 [7366656], P(('outer', 'middle', 'inner'))
- output 2: float32 [7366656], P(('outer', 'middle', 'inner'))
- output 3: float32 [7366656], P(('outer', 'middle', 'inner'))
- output 4: bfloat16 [32768, 128], replicated
- output 5: bfloat16 [16, 128, 512], replicated
- output 6: bfloat16 [16, 128, 512], replicated
- output 7: bfloat16 [16, 512, 128], replicated
- output 8: bfloat16 [16, 1664], replicated
- output 9: bfloat16 [8, 1841664], P(('outer', 'middle', 'inner'))
All inputs are finite; a program needn't handle non-finite values.
Results may differ from a plain program's by a relative error of at most 0.001.
Values are sent between devices in bfloat16 or wider.
A program may use at most 1 GiB of HBM per device.

v0:
```python
import math
import jax
import jax.numpy as jnp
from jax import lax
from jax.sharding import PartitionSpec as P

MESH_AXES = ('outer', 'middle', 'inner')
ADAM_BETA1 = 0.9
ADAM_BETA2 = 0.98
ADAM_EPS = 1e-9
LEARN_RATE = 0.05
ADAM_STEP = 3


def adam_update(grad_mean, m_old, v_old, w_old):
    m_new = ADAM_BETA1 * m_old + (1.0 - ADAM_BETA1) * grad_mean
    v_new = ADAM_BETA2 * v_old + (1.0 - ADAM_BETA2) * (grad_mean * grad_mean)
    m_hat = m_new / (1.0 - ADAM_BETA1 ** ADAM_STEP)
    v_hat = v_new / (1.0 - ADAM_BETA2 ** ADAM_STEP)
    w_new = w_old - LEARN_RATE * m_hat / (jnp.sqrt(v_hat) + ADAM_EPS)
    return m_new, v_new, w_new


def split_tensors(flat_values, shape_list):
    pieces = []
    offset = 0
    for shape in shape_list:
        count = math.prod(shape)
        pieces.append(flat_values[offset:offset + count].reshape(shape))
        offset += count
    return pieces


def own_chip_block(w_tensors, chip_index, num_chips):
    embed_rows = w_tensors[0].shape[0] // num_chips
    block_list = [lax.dynamic_slice_in_dim(w_tensors[0], chip_index * embed_rows, embed_rows, axis=0).reshape(-1)]
    for tensor in w_tensors[1:]:
        block_rows = tensor.shape[1] // num_chips
        block_list.append(lax.dynamic_slice_in_dim(tensor, chip_index * block_rows, block_rows, axis=1).reshape(-1))
    return jnp.concatenate(block_list)[None, :]


def solution(mesh):
    num_devices = mesh.shape['outer'] * mesh.shape['middle'] * mesh.shape['inner']
    num_chips = num_devices // 2

    def local_step(g_embed, g_attn, g_ffn_in, g_ffn_out, g_vec, m_shard, v_shard, w_shard):
        grad_list = (g_embed, g_attn, g_ffn_in, g_ffn_out, g_vec)
        local_flat = jnp.concatenate([gradient.reshape(-1) for gradient in grad_list])
        grad_mean = lax.psum_scatter(local_flat, MESH_AXES, scatter_dimension=0, tiled=True) / num_devices
        m_new, v_new, w_new = adam_update(grad_mean, m_shard, v_shard, w_shard)
        w_full = lax.all_gather(w_new.astype(jnp.bfloat16), MESH_AXES, axis=0, tiled=True)
        w_tensors = split_tensors(w_full, [gradient.shape[1:] for gradient in grad_list])
        device_index = (lax.axis_index('outer') * mesh.shape['middle'] + lax.axis_index('middle')) * mesh.shape['inner'] + lax.axis_index('inner')
        w_chip = own_chip_block(w_tensors, device_index // 2, num_chips)
        return (m_new, v_new, w_new) + tuple(w_tensors) + (w_chip,)

    return jax.shard_map(local_step, mesh=mesh, in_specs=(P(MESH_AXES),) * 8, out_specs=(P(MESH_AXES),) * 3 + (P(),) * 5 + (P(MESH_AXES),), check_vma=False)
```

profile of v0, /device:TPU:0, one launch (start us, length us, event | category | flops | bytes accessed | tf_op | source)
XLA Modules:
  0.0 935.1 jit_solution(4522826075601583223)
XLA Ops:
  7.2 11.8 %bitcast_dynamic-update-slice_fusion = f32[7366656]{0:T(1024)} fusion(f32[1,32768,128]{2,1,0:T(8,128)} %param.8), kind=kLoop, calls=%fused_computation | loop fusion | bytes 33554432
  19.1 3.1 copy.17
  22.2 3.1 copy.18
  25.3 4.6 constant_dynamic-update-slice_fusion.3
  29.9 2.4 constant_dynamic-update-slice_fusion.2
  32.3 1.3 copy-done.4
  33.6 2.3 constant_dynamic-update-slice_fusion.1
  35.9 0.6 constant_dynamic-update-slice_fusion
  36.5 0.2 all-gather.3.cloned.1.call-start
  36.7 345.8 %all-reduce.3.cloned.1.call-done = f32[7366656]{0:T(1024)} async-done(((f32[7366656]{0:T(1024)}), f32[7366656]{0:T(1024)}) %all-reduce.3.cloned.1.call-update) | async-done | bytes 29466640
  382.5 9.2 fusion
  391.7 21.8 %reshape.83 = bf16[1,1,920832]{2,1,0:T(2,128)(2,1)} reshape(bf16[920832]{0:T(1024)(128)(2,1)S(1)} %get-tuple-element.9) | data formatting | bytes 3683328
  413.5 138.0 %all-gather.3.cloned.1.call-done = bf16[8,1,920832]{2,1,0:T(2,128)(2,1)} async-done(((bf16[1,1,920832]{2,1,0:T(2,128)(2,1)}), bf16[8,1,920832]{2,1,0:T(2,128)(2,1)}) %all-gather.3.cloned.1.call-update) | async-done | bytes 14733328 | tf_op jit(solution)/shard_map/all_gather | solution.py:52
  551.5 313.0 %reduce = bf16[8,920832]{1,0:T(8,128)(2,1)} reduce(bf16[8,1,920832]{2,1,0:T(2,128)(2,1)} %all-gather.3.cloned.1.call-done, bf16[]{:T(256)} %constant.70), dimensions={1}, to_apply=%all-gather.reduce_sub_computation | reduce | bytes 29466626 | tf_op jit(solution)/shard_map/all_gather | solution.py:52
  864.5 32.8 %reshape.84 = bf16[7366656]{0:T(1024)(128)(2,1)} reshape(bf16[8,920832]{1,0:T(8,128)(2,1)} %reduce) | data formatting | bytes 29466624
  897.3 7.4 slice_bitcast_fusion
  904.7 3.3 copy-done
  908.0 2.4 fusion.1
  910.4 4.3 reshape.74
  914.8 2.5 reshape.75
  917.4 1.3 constant_dynamic-slice_fusion.2
  919.3 1.7 bitcast_dynamic-update-slice_fusion.1
  921.2 1.1 constant_dynamic-slice_fusion.1
  922.3 5.8 broadcast_in_dim.3
  (27 shorter events, 1.0 us)
Async XLA Ops:
  7.2 375.3 %all-reduce.3.cloned.1.call-start = ((), (), s32[]{:S(2)}) async-start(), calls=%async_computation.1 | async-start | bytes 58933248
  7.2 11.9 %copy-start.2 = (f32[1,16,128,512]{3,2,1,0:T(8,128)S(1)}, f32[1,16,128,512]{3,2,1,0:T(8,128)}, u32[]{:S(2)}) copy-start(f32[1,16,128,512]{3,2,1,0:T(8,128)} %param.9) | copy-start | bytes 12582916
  19.1 3.1 copy-start.3
  22.2 3.1 copy-start.5
  25.3 4.6 copy-start.1
  29.9 3.7 copy-start.4
  36.5 515.0 %all-gather.3.cloned.1.call-start = ((), (), s32[]{:S(2)}) async-start(), calls=%async_computation | async-start | bytes 33149952 | tf_op jit(solution)/shard_map/all_gather | solution.py:52
  897.3 10.7 %copy-start = (bf16[7366656]{0:T(1024)(128)(2,1)S(1)}, bf16[7366656]{0:T(1024)(128)(2,1)}, u32[]{:S(2)}) copy-start(bf16[7366656]{0:T(1024)(128)(2,1)} %reshape.84) | copy-start | bytes 44199940
  910.4 6.9 slice-start
  917.4 3.7 copy-start.6
Sparse Core Ops, SparseCore 0:
  36.6 345.8 all-reduce.2
  413.6 137.8 all-gather.2
where the time goes:
time: 939 us; the launch traced here: 935 us
  waiting for transfers between devices  484 us (52%)
  other arithmetic  322 us (34%)
  local copies, waits for them, and re-layouts  115 us (12%)
  between operations  14.4 us (2%)
    unnamed x3, waiting for transfers between devices  346 us
    all_gather x1, other arithmetic, local_step(): lax.all_gather(w_new.astype(jnp.bfloat16), MESH_AXES, axis=0, tiled=True)  313 us
    all_gather x1, waiting for transfers between devices, local_step(): lax.all_gather(w_new.astype(jnp.bfloat16), MESH_AXES, axis=0, tiled=True)  138 us
    unnamed x28, local copies, waits for them, and re-layouts  88.7 us
  transfers between devices with their start and end apart: 2, of which 2 were waited for; matrix products, arithmetic and copies ran while one was open for 0% of the time, Pallas kernels for 0%

commit v1 on v0

v1 whole, which is shorter than its diff:
```python
import functools
import math
import jax
import jax.numpy as jnp
from jax import lax
from jax.experimental import pallas as pl
from jax.experimental.pallas import tpu as pltpu
from jax.sharding import PartitionSpec as P

MESH_AXES = ('outer', 'middle', 'inner')
ADAM_BETA1 = 0.9
ADAM_BETA2 = 0.98
ADAM_EPS = 1e-9
LEARN_RATE = 0.05
ADAM_STEP = 3

MESH = pl.DeviceIdType.MESH
F32 = jnp.float32
BF16 = jnp.bfloat16

LANES = 128
GROUP = 32
ROWS = 7366656 // LANES
SLICE_ROWS = ROWS // 8
CHUNKS = 19
CHUNK_GROUPS = 12
CHUNK = CHUNK_GROUPS * GROUP
HALF = CHUNK // 2
WINDOW = CHUNKS * CHUNK
LAST_ROWS = SLICE_ROWS - (CHUNKS - 1) * CHUNK
FRONT = 96
BOUNDS = (0, 1024, 1280, 1536, 1792, 1799)
PERMUTED = (1024, 1536)
START_MAX = BOUNDS[-1] - WINDOW // GROUP


def window_start(device):
    return min(SLICE_ROWS * device // GROUP, START_MAX)


def window_start_traced(device):
    return jnp.minimum(lax.div(device * SLICE_ROWS, GROUP), START_MAX)


def split_chunks():
    found = []
    for device in range(8):
        for chunk in range(CHUNKS):
            first = window_start(device) + chunk * CHUNK_GROUPS
            for tensor in range(4):
                edge = BOUNDS[tensor + 1]
                if first < edge < first + CHUNK_GROUPS:
                    found.append((first, tensor, edge - first))
    return tuple(found)


SPLITS = split_chunks()


def step_kernel(e_ref, a_ref, f1_ref, f2_ref, b_ref, m_ref, v_ref, w_ref,
                m_out, v_out, w_out, wg_ref,
                acc, local, p1x, p1y, p2x, p2y, gflat, wflat, wbf, m_in, m_new,
                local_sem, d2d_send, d2d_recv, p1_send, p1x_recv, p1y_recv, p2_send, p2x_recv, p2y_recv,
                in_sem, out_sem, ag_send, agx_recv, agy_recv, relay_send, relx_recv, rely_recv, fwd_send, fwd_recv):
    o, m, i = lax.axis_index('outer'), lax.axis_index('middle'), lax.axis_index('inner')
    x_dev, y_dev, p_dev = (o, 1 - m, i), (1 - o, m, i), (o, m, 1 - i)
    places = ((o, m), (o, 1 - m), (1 - o, m), (1 - o, 1 - m))
    mine = [(po * 2 + pm) * 2 + i for po, pm in places]
    theirs = [(po * 2 + pm) * 2 + (1 - i) for po, pm in places]
    start = window_start_traced(mine[0])
    shift = mine[0] * SLICE_ROWS - start * GROUP
    tensors = (e_ref, a_ref, f1_ref, f2_ref, b_ref)

    barrier = pltpu.get_barrier_semaphore()
    for device in (x_dev, y_dev, p_dev):
        pl.semaphore_signal(barrier, inc=1, device_id=device, device_id_type=MESH)
    pl.semaphore_wait(barrier, 3)

    def remote(src, dst, send, recv, device):
        pltpu.make_async_remote_copy(src_ref=src, dst_ref=dst, send_sem=send, recv_sem=recv, device_id=device, device_id_type=MESH).start()

    def drain(ref, sem):
        pltpu.make_async_copy(ref, ref, sem).wait()

    def load_chunk(device, chunk, copy):
        first = window_start_traced(device) + chunk * CHUNK_GROUPS
        for tensor in range(4):
            @pl.when((first >= BOUNDS[tensor]) & (first + CHUNK_GROUPS <= BOUNDS[tensor + 1]))
            def _():
                row = pl.multiple_of((first - BOUNDS[tensor]) * GROUP, GROUP)
                copy(tensors[tensor].at[pl.ds(row, CHUNK)], 0, CHUNK)
        for known, tensor, count in SPLITS:
            @pl.when(first == known)
            def _():
                head = count * GROUP
                copy(tensors[tensor].at[pl.ds((known - BOUNDS[tensor]) * GROUP, head)], 0, head)
                copy(tensors[tensor + 1].at[pl.ds(0, CHUNK - head)], head, CHUNK - head)

    def issue_gradients(chunk):
        slot = lax.rem(chunk, 3)
        base = pl.multiple_of(chunk * CHUNK, CHUNK)
        for j in (3, 1, 2, 0):
            load_chunk(theirs[j], chunk, lambda src, off, size: remote(
                src, acc.at[j, pl.ds(pl.multiple_of(base + off, GROUP), size)], d2d_send, d2d_recv.at[chunk], p_dev))
            load_chunk(mine[j], chunk, lambda src, off, size: pltpu.make_async_copy(
                src, local.at[slot, j, pl.ds(off, size)], local_sem.at[slot]).start())

    def add_rows(j, base, count, term):
        @pl.loop(0, count // GROUP)
        def _(r):
            off = pl.multiple_of(r * GROUP, GROUP)
            at = pl.ds(pl.multiple_of(base + off, GROUP), GROUP)
            acc[j, at] = acc[j, at] + term(off)

    def first_phase(chunk):
        slot = lax.rem(chunk, 3)
        base = pl.multiple_of(chunk * CHUNK, CHUNK)
        second = pl.multiple_of(base + HALF, HALF)
        drain(local.at[slot], local_sem.at[slot])
        drain(local.at[0], d2d_recv.at[chunk])
        add_rows(1, base, HALF, lambda off: local[slot, 1, pl.ds(off, GROUP)])
        add_rows(2, second, HALF, lambda off: local[slot, 2, pl.ds(HALF + off, GROUP)])
        add_rows(3, base, CHUNK, lambda off: local[slot, 3, pl.ds(off, GROUP)])
        remote(acc.at[1, pl.ds(base, HALF)], p1x.at[chunk, 0], p1_send.at[0], p1x_recv.at[chunk], x_dev)
        remote(acc.at[2, pl.ds(second, HALF)], p1y.at[chunk, 0], p1_send.at[1], p1y_recv.at[chunk], y_dev)
        remote(acc.at[3, pl.ds(base, HALF)], p1x.at[chunk, 1], p1_send.at[0], p1x_recv.at[chunk], x_dev)
        remote(acc.at[3, pl.ds(second, HALF)], p1y.at[chunk, 1], p1_send.at[1], p1y_recv.at[chunk], y_dev)
        add_rows(2, base, HALF, lambda off: local[slot, 2, pl.ds(off, GROUP)])
        add_rows(1, second, HALF, lambda off: local[slot, 1, pl.ds(HALF + off, GROUP)])
        add_rows(0, base, CHUNK, lambda off: local[slot, 0, pl.ds(off, GROUP)])

    def second_phase(chunk):
        base = pl.multiple_of(chunk * CHUNK, CHUNK)
        second = pl.multiple_of(base + HALF, HALF)
        drain(p1x.at[chunk], p1x_recv.at[chunk])
        add_rows(2, base, HALF, lambda off: p1x[chunk, 1, pl.ds(off, GROUP)])
        drain(p1y.at[chunk], p1y_recv.at[chunk])
        add_rows(1, second, HALF, lambda off: p1y[chunk, 1, pl.ds(off, GROUP)])
        remote(acc.at[2, pl.ds(base, HALF)], p2y.at[chunk], p2_send.at[0], p2y_recv.at[chunk], y_dev)
        remote(acc.at[1, pl.ds(second, HALF)], p2x.at[chunk], p2_send.at[1], p2x_recv.at[chunk], x_dev)
        add_rows(0, base, HALF, lambda off: p1x[chunk, 0, pl.ds(off, GROUP)])
        add_rows(0, second, HALF, lambda off: p1y[chunk, 0, pl.ds(off, GROUP)])

    def is_permuted(group):
        return (group >= PERMUTED[0]) & (group < PERMUTED[1])

    def last_phase(chunk):
        base = pl.multiple_of(chunk * CHUNK, CHUNK)
        first = start + chunk * CHUNK_GROUPS
        for part, (arrived, sem) in enumerate(((p2y, p2y_recv), (p2x, p2x_recv))):
            drain(arrived.at[chunk], sem.at[chunk])

            @pl.loop(0, HALF // GROUP)
            def _(r):
                off = pl.multiple_of(r * GROUP, GROUP)
                row = pl.multiple_of(base + part * HALF + off, GROUP)
                total = acc[0, pl.ds(row, GROUP)] + arrived[chunk, pl.ds(off, GROUP)]
                permuted = is_permuted(first + part * (HALF // GROUP) + r)

                @pl.when(permuted)
                def _():
                    for tile in range(4):
                        gflat[pl.ds(row + tile, 8, stride=4)] = total[8 * tile:8 * tile + 8]

                @pl.when(jnp.logical_not(permuted))
                def _():
                    gflat[pl.ds(row, GROUP)] = total

    def state_copies(block, size):
        slot = lax.rem(block, 2)
        at = pl.ds(pl.multiple_of(block * CHUNK, CHUNK), size)
        loads = [pltpu.make_async_copy(ref.at[at], m_in.at[slot, q, pl.ds(0, size)], in_sem.at[slot, q])
                 for q, ref in enumerate((m_ref, v_ref, w_ref))]
        stores = [pltpu.make_async_copy(m_new.at[slot, q, pl.ds(0, size)], ref.at[at], out_sem.at[slot, q])
                  for q, ref in enumerate((m_out, v_out, w_out))]
        return loads, stores

    def for_block(block, action):
        @pl.when(block < CHUNKS - 1)
        def _():
            action(*state_copies(block, CHUNK))

        @pl.when(block == CHUNKS - 1)
        def _():
            action(*state_copies(block, LAST_ROWS))

    def start_loads(loads, stores):
        for copy in loads:
            copy.start()

    def wait_loads(loads, stores):
        for copy in loads:
            copy.wait()

    def start_stores(loads, stores):
        for copy in stores:
            copy.start()

    def wait_stores(loads, stores):
        for copy in stores:
            copy.wait()

    def adam(block):
        slot = lax.rem(block, 2)
        base = pl.multiple_of(block * CHUNK, CHUNK)
        for_block(block, wait_loads)

        @pl.when(block >= 2)
        def _():
            for_block(block - 2, wait_stores)

        @pl.loop(0, CHUNK_GROUPS)
        def _(r):
            off = pl.multiple_of(r * GROUP, GROUP)
            at = pl.ds(off, GROUP)
            grad = gflat[pl.ds(base + off + shift, GROUP)] / 8
            m_val = ADAM_BETA1 * m_in[slot, 0, at] + (1.0 - ADAM_BETA1) * grad
            v_val = ADAM_BETA2 * m_in[slot, 1, at] + (1.0 - ADAM_BETA2) * (grad * grad)
            m_hat = m_val / (1.0 - ADAM_BETA1 ** ADAM_STEP)
            v_hat = v_val / (1.0 - ADAM_BETA2 ** ADAM_STEP)
            w_val = m_in[slot, 2, at] - LEARN_RATE * m_hat / (jnp.sqrt(v_hat) + ADAM_EPS)
            m_new[slot, 0, at] = m_val
            m_new[slot, 1, at] = v_val
            m_new[slot, 2, at] = w_val
            wflat[pl.ds(pl.multiple_of(FRONT + base + off, GROUP), GROUP)] = w_val

        for_block(block, start_stores)

        @pl.loop(0, CHUNK_GROUPS)
        def _(r):
            row = pl.multiple_of(base + r * GROUP, GROUP)
            source = FRONT + row - shift
            permuted = is_permuted(start + block * CHUNK_GROUPS + r)

            @pl.when(permuted)
            def _():
                tiles = [wflat[pl.ds(source + tile, 8, stride=4)] for tile in range(4)]
                wbf[pl.ds(row, GROUP)] = jnp.concatenate(tiles, axis=0).astype(BF16)

            @pl.when(jnp.logical_not(permuted))
            def _():
                wbf[pl.ds(row, GROUP)] = wflat[pl.ds(source, GROUP)].astype(BF16)

        at = pl.ds(base, CHUNK)
        remote(wbf.at[at], wg_ref.at[mine[0], at], ag_send.at[0], agx_recv.at[block], x_dev)
        remote(wbf.at[at], wg_ref.at[mine[0], at], ag_send.at[1], agy_recv.at[block], y_dev)
        remote(wbf.at[at], wg_ref.at[mine[0], at], fwd_send.at[0], fwd_recv.at[0], p_dev)
        pltpu.make_async_copy(wbf.at[at], wg_ref.at[mine[0], at], ag_send.at[2]).start()

    def relay(chunk):
        base = pl.multiple_of(chunk * CHUNK, CHUNK)
        at, head, tail = pl.ds(base, CHUNK), pl.ds(base, HALF), pl.ds(pl.multiple_of(base + HALF, HALF), HALF)
        drain(wbf.at[pl.ds(0, CHUNK)], agx_recv.at[chunk])
        remote(wg_ref.at[mine[1], head], wg_ref.at[mine[1], head], relay_send.at[0], rely_recv.at[chunk], y_dev)
        remote(wg_ref.at[mine[1], at], wg_ref.at[mine[1], at], fwd_send.at[1], fwd_recv.at[1], p_dev)
        drain(wbf.at[pl.ds(0, CHUNK)], agy_recv.at[chunk])
        remote(wg_ref.at[mine[2], tail], wg_ref.at[mine[2], tail], relay_send.at[1], relx_recv.at[chunk], x_dev)
        remote(wg_ref.at[mine[2], at], wg_ref.at[mine[2], at], fwd_send.at[2], fwd_recv.at[2], p_dev)

    def forward(chunk):
        base = pl.multiple_of(chunk * CHUNK, CHUNK)
        at = pl.ds(base, CHUNK)
        drain(wbf.at[pl.ds(0, HALF)], rely_recv.at[chunk])
        drain(wbf.at[pl.ds(0, HALF)], relx_recv.at[chunk])
        remote(wg_ref.at[mine[3], at], wg_ref.at[mine[3], at], fwd_send.at[3], fwd_recv.at[3], p_dev)

    issue_gradients(0)
    issue_gradients(1)

    stages = ((0, first_phase), (1, second_phase), (2, last_phase), (3, adam), (5, relay), (6, forward))

    @pl.loop(0, CHUNKS + stages[-1][0])
    def _(t):
        @pl.when(t + 2 < CHUNKS)
        def _():
            issue_gradients(t + 2)

        @pl.when((t >= 2) & (t - 2 < CHUNKS))
        def _():
            for_block(t - 2, start_loads)

        for lag, stage in stages:
            @pl.when((t >= lag) & (t - lag < CHUNKS))
            def _():
                stage(t - lag)

    for block in (CHUNKS - 2, CHUNKS - 1):
        for_block(block, wait_stores)
    drain(acc, d2d_send)
    for q in range(2):
        drain(acc.at[0], p1_send.at[q])
        drain(acc.at[0, pl.ds(0, WINDOW // 2)], p2_send.at[q])
        drain(wbf.at[pl.ds(0, WINDOW // 2)], relay_send.at[q])
    for q in range(3):
        drain(wbf, ag_send.at[q])
    for q in range(4):
        drain(wbf, fwd_send.at[q])
        drain(wbf, fwd_recv.at[q])


def step_call(tensors, state):
    hbm = pl.BlockSpec(memory_space=pl.ANY)
    dma = pltpu.SemaphoreType.DMA
    flat = jax.ShapeDtypeStruct((SLICE_ROWS, LANES), F32)
    return pl.pallas_call(
        step_kernel,
        name='adam_step',
        out_shape=(flat, flat, flat, jax.ShapeDtypeStruct((8, WINDOW, LANES), BF16)),
        in_specs=[hbm] * 8,
        out_specs=[hbm] * 4,
        scratch_shapes=[
            pltpu.VMEM((4, WINDOW, LANES), F32),
            pltpu.VMEM((3, 4, CHUNK, LANES), F32),
            pltpu.VMEM((CHUNKS, 2, HALF, LANES), F32),
            pltpu.VMEM((CHUNKS, 2, HALF, LANES), F32),
            pltpu.VMEM((CHUNKS, HALF, LANES), F32),
            pltpu.VMEM((CHUNKS, HALF, LANES), F32),
            pltpu.VMEM((WINDOW + 128, LANES), F32),
            pltpu.VMEM((WINDOW + FRONT, LANES), F32),
            pltpu.VMEM((WINDOW, LANES), BF16),
            pltpu.VMEM((2, 3, CHUNK, LANES), F32),
            pltpu.VMEM((2, 3, CHUNK, LANES), F32),
            dma((3,)), dma, dma((CHUNKS,)), dma((2,)), dma((CHUNKS,)), dma((CHUNKS,)), dma((2,)), dma((CHUNKS,)), dma((CHUNKS,)),
            dma((2, 3)), dma((2, 3)), dma((3,)), dma((CHUNKS,)), dma((CHUNKS,)), dma((2,)), dma((CHUNKS,)), dma((CHUNKS,)),
            dma((4,)), dma((4,)),
        ],
        compiler_params=pltpu.CompilerParams(collective_id=0, has_side_effects=True, vmem_limit_bytes=56 * 1024 * 1024),
    )(*tensors, *state)


LAYERS = 16
CHIP_ROWS = 8192 + 3 * 2048


def place_kernel(wg_ref, e_ref, a_ref, f1_ref, f2_ref, b_ref, chip_ref, full, edge, wide, block, in_sem, edge_sem, out_sem, chip_sem):
    chip = lax.axis_index('outer') * 2 + lax.axis_index('middle')
    firsts = [SLICE_ROWS * d // GROUP for d in range(8)] + [BOUNDS[-1]]
    loads = []
    for d in range(8):
        first, last = firsts[d], firsts[d + 1]
        src = wg_ref.at[d, pl.ds((first - window_start(d)) * GROUP, (last - first) * GROUP)]
        loads.append(pltpu.make_async_copy(src, full.at[pl.ds(first * GROUP, (last - first) * GROUP)], in_sem.at[d]))
        loads[-1].start()
    edges = []
    for d in range(1, 8):
        src = wg_ref.at[d - 1, pl.ds((firsts[d] - window_start(d - 1)) * GROUP, GROUP)]
        edges.append(pltpu.make_async_copy(src, edge.at[d - 1], edge_sem.at[d - 1]))
        edges[-1].start()
    for d in range(8):
        loads[d].wait()
        if d:
            edges[d - 1].wait()
            keep = SLICE_ROWS * d - firsts[d] * GROUP
            row = lax.broadcasted_iota(jnp.int32, (GROUP, LANES), 0)
            if PERMUTED[0] <= firsts[d] < PERMUTED[1]:
                row = 4 * (row % 8) + row // 8
            at = pl.ds(firsts[d] * GROUP, GROUP)
            full[at] = jnp.where(row < keep, edge[d - 1].astype(F32), full[at].astype(F32)).astype(BF16)
    outs = []
    for q, ref in enumerate((e_ref, a_ref, f1_ref, f2_ref, b_ref)):
        size = ref.shape[0]
        outs.append(pltpu.make_async_copy(full.at[pl.ds(BOUNDS[q] * GROUP, size)], ref, out_sem.at[q]))
        outs[-1].start()
    embed = pltpu.make_async_copy(full.at[pl.ds(pl.multiple_of(chip * 8192, GROUP), 8192)], chip_ref.at[pl.ds(0, 8192)], chip_sem.at[0])
    embed.start()

    @pl.loop(0, LAYERS)
    def _(layer):
        row = pl.multiple_of(BOUNDS[3] * GROUP + layer * 512 + chip * 128, GROUP)
        pltpu.make_async_copy(full.at[pl.ds(row, 128)], chip_ref.at[pl.ds(pl.multiple_of(8192 + 4096 + layer * 128, 128), 128)], chip_sem.at[1]).start()

    for q in range(2):
        @pl.loop(0, LAYERS * 4)
        def _(r):
            row = pl.multiple_of(BOUNDS[1 + q] * GROUP + (r // 4) * 512 + chip * 128 + (r % 4) * GROUP, GROUP)
            group = full[pl.ds(row, GROUP)].astype(F32)
            for tile in range(4):
                wide[r % 4, pl.ds(tile, 8, stride=4)] = group[8 * tile:8 * tile + 8]
            block[q, pl.ds(pl.multiple_of(r * GROUP, GROUP), GROUP)] = wide[r % 4].astype(BF16)
        outs.append(pltpu.make_async_copy(block.at[q], chip_ref.at[pl.ds(8192 + q * 2048, 2048)], chip_sem.at[2 + q]))
        outs[-1].start()
    for copy in outs:
        copy.wait()
    embed.wait()
    pltpu.make_async_copy(block.at[0], chip_ref.at[pl.ds(8192 + 4096, 2048)], chip_sem.at[1]).wait()


def place_call(gathered):
    hbm = pl.BlockSpec(memory_space=pl.ANY)
    dma = pltpu.SemaphoreType.DMA
    sizes = (32768, 8192, 8192, 8192, 208, CHIP_ROWS)
    return pl.pallas_call(
        place_kernel,
        name='place_weights',
        out_shape=tuple(jax.ShapeDtypeStruct((size, LANES), BF16) for size in sizes),
        in_specs=[hbm],
        out_specs=[hbm] * 6,
        scratch_shapes=[
            pltpu.VMEM((BOUNDS[-1] * GROUP, LANES), BF16),
            pltpu.VMEM((7, GROUP, LANES), BF16),
            pltpu.VMEM((4, GROUP, LANES), F32),
            pltpu.VMEM((2, 2048, LANES), BF16),
            dma((8,)), dma((7,)), dma((5,)), dma((4,)),
        ],
        compiler_params=pltpu.CompilerParams(vmem_limit_bytes=24 * 1024 * 1024),
    )(gathered)


def to_tiles(tensor):
    return tensor.reshape(256, 8, 4, LANES).transpose(0, 2, 1, 3).reshape(8192, LANES)


def from_tiles(rows):
    return rows.reshape(256, 4, 8, LANES).transpose(0, 2, 1, 3).reshape(16, 128, 512)


def solution(mesh):
    def local_step(g_embed, g_attn, g_ffn_in, g_ffn_out, g_vec, m_shard, v_shard, w_shard):
        vec_rows = jnp.pad(g_vec.reshape(208, LANES), ((0, 16), (0, 0)))
        tensors = (g_embed.reshape(32768, LANES), to_tiles(g_attn), to_tiles(g_ffn_in), g_ffn_out.reshape(8192, LANES), vec_rows)
        state = [shard.reshape(SLICE_ROWS, LANES) for shard in (m_shard, v_shard, w_shard)]
        m_new, v_new, w_new, gathered = step_call(tensors, state)
        embed, attn, ffn_in, ffn_out, vec, chip_rows = place_call(gathered)
        wb_vec = vec.reshape(16, 1664)
        chip = lax.axis_index('outer') * 2 + lax.axis_index('middle')
        vec_block = lax.dynamic_slice_in_dim(wb_vec, chip * 416, 416, axis=1).reshape(-1)
        w_chip = jnp.concatenate([chip_rows.reshape(-1), vec_block])[None, :]
        return (m_new.reshape(-1), v_new.reshape(-1), w_new.reshape(-1), embed, from_tiles(attn), from_tiles(ffn_in),
                ffn_out.reshape(16, 512, 128), wb_vec, w_chip)

    return jax.shard_map(local_step, mesh=mesh, in_specs=(P(MESH_AXES),) * 8, out_specs=(P(MESH_AXES),) * 3 + (P(),) * 5 + (P(MESH_AXES),), check_vma=False)
```

time: 939 us -> 233 us (0.25)
  waiting for transfers between devices: 484 us -> 0 us
  other arithmetic: 322 us -> 9.61 us
  Pallas kernels: 0 us -> 198 us
  local copies, waits for them, and re-layouts: 115 us -> 23.5 us
  between operations: 14.4 us -> 0.73 us
    unnamed x3 -> x0, waiting for transfers between devices: 346 us -> none
    all_gather x1 -> x0, other arithmetic: 313 us -> none  [local_step(): lax.all_gather(w_new.astype(jnp.bfloat16), MESH_AXES, axis=0, tiled=True)]
    pallas_call x0 -> x2, Pallas kernels: none -> 198 us  [the longest x1 192 us: step_call(): pl.pallas_call(step_kernel, name='adam_step', out_shape=(flat, flat, flat...]
    all_gather x1 -> x0, waiting for transfers between devices: 138 us -> none  [local_step(): lax.all_gather(w_new.astype(jnp.bfloat16), MESH_AXES, axis=0, tiled=True)]
    unnamed x28 -> x15, local copies, waits for them, and re-layouts: 88.7 us -> 15.9 us
    slice x4 -> x0, local copies, waits for them, and re-layouts: 9.87 us -> none  [split_tensors(): pieces.append(flat_values[offset:offset + count].reshape(shape))]
    concatenate x0 -> x1, other arithmetic: none -> 9.61 us  [local_step(): w_chip = jnp.concatenate([chip_rows.reshape(-1), vec_block])[None, :]]
  transfers between devices with their start and end apart: 2 -> 0, of which waited for: 2 -> 0; matrix products, arithmetic and copies ran while one was open for 0% -> 0% of each run, Pallas kernels for 0% -> 0%
where the time goes in v1:
time: 233 us; the launch traced here: 232 us
  Pallas kernels  198 us (85%)
  local copies, waits for them, and re-layouts  23.5 us (10%)
  other arithmetic  9.61 us (4%)
    pallas_call x1, Pallas kernels, step_call(): pl.pallas_call(step_kernel, name='adam_step', out_shape=(flat, flat, flat...  192 us
    unnamed x15, local copies, waits for them, and re-layouts  15.9 us
    concatenate x1, other arithmetic, local_step(): w_chip = jnp.concatenate([chip_rows.reshape(-1), vec_block])[None, :]  9.61 us
    pallas_call x1, Pallas kernels, place_call(): pl.pallas_call(place_kernel, name='place_weights', out_shape=tuple((jax.S...  6.75 us
    broadcast_in_dim x1, local copies, waits for them, and re-layouts, local_step(): w_chip = jnp.concatenate([chip_rows.reshape(-1), vec_block])[None, :]  5.77 us

profile of v1, /device:TPU:0, one launch (start us, length us, event | category | flops | bytes accessed | tf_op | source)
XLA Modules:
  0.0 232.3 jit_solution(8522295128940593133)
XLA Ops:
  0.6 0.9 reshape.87
  1.5 0.7 pad.4.b_ref
  2.2 191.7 %adam_step.1 = (f32[7194,128]{1,0:T(8,128)}, f32[7194,128]{1,0:T(8,128)}, f32[7194,128]{1,0:T(8,128)}, bf16[8,7296,128]{2,1,0:T(8,128)(2,1)}) custom-call(f32[32768,128]{1,0:T(8,128)} %bitcast.31, f32[8192,128]{1,0:T(8,128)} %bitcast.32, f32[8192,128]{1,0:T(8,128)} %bitcast.33, f32[8192,128]{1,0:T(8,128)} %bitcast.34, f32[224,128]{1,0:T(8,128)} %pad.4.b_ref, ...), custom_call_target="tpu_custom_call" | custom-call | tf_op jit(solution)/shard_map/adam_step/pallas_call | solution.py:305
  193.9 0.0 copy-start
  194.0 5.2 %copy-done = bf16[8,7296,128]{2,1,0:T(8,128)(2,1)S(1)} copy-done((bf16[8,7296,128]{2,1,0:T(8,128)(2,1)S(1)}, bf16[8,7296,128]{2,1,0:T(8,128)(2,1)}, u32[]{:S(2)}) %copy-start) | copy-done | bytes 14942232
  199.2 6.8 %place_weights.1 = (bf16[32768,128]{1,0:T(8,128)(2,1)}, bf16[8192,128]{1,0:T(8,128)(2,1)}, bf16[8192,128]{1,0:T(8,128)(2,1)}, bf16[8192,128]{1,0:T(8,128)(2,1)},...) custom-call(bf16[8,7296,128]{2,1,0:T(8,128)(2,1)S(1)} %copy-done), custom_call_target="tpu_custom_call" | custom-call | tf_op jit(solution)/shard_map/place_weights/pallas_call | solution.py:392
  206.0 0.0 copy-start.1
  206.0 1.8 copy-done.1
  207.8 0.1 reshape.99
  207.9 0.0 copy-start.5
  207.9 0.1 constant_dynamic-slice_fusion
  208.0 0.1 reshape.101
  208.1 9.6 %pad_maximum_fusion = bf16[1841664]{0:T(1024)(128)(2,1)S(1)} fusion(bf16[6656]{0:T(1024)(128)(2,1)S(1)} %reshape.101, bf16[1835008]{0:T(1024)(128)(2,1)} %bitcast.30), kind=kLoop, calls=%fused_computation | loop fusion | flops 7366656 | bytes 7366656 | tf_op jit(solution)/shard_map/concatenate | solution.py:427
  217.7 0.0 copy-done.5
  217.7 0.0 copy-start.4
  217.7 5.8 %broadcast_in_dim.3 = bf16[1,1841664]{1,0:T(2,128)(2,1)} reshape(bf16[1841664]{0:T(1024)(128)(2,1)S(1)} %pad_maximum_fusion) | data formatting | bytes 7366656 | tf_op jit(solution)/shard_map/broadcast_in_dim | solution.py:427
  223.5 0.0 copy-done.4
  223.5 0.0 copy-start.3
  223.5 2.1 copy.20
  225.6 1.2 copy-done.3
  226.9 0.0 copy-start.2
  226.9 2.1 copy.21
  229.0 1.2 copy-done.2
  230.3 2.1 copy.22
Async XLA Ops:
  193.9 5.2 %copy-start = (bf16[8,7296,128]{2,1,0:T(8,128)(2,1)S(1)}, bf16[8,7296,128]{2,1,0:T(8,128)(2,1)}, u32[]{:S(2)}) copy-start(bf16[8,7296,128]{2,1,0:T(8,128)(2,1)} %get-tuple-element.22.wg_ref) | copy-start | bytes 44826628
  206.0 1.8 copy-start.1
  207.9 9.8 %copy-start.5 = (bf16[16,1664]{1,0:T(8,128)(2,1)}, bf16[16,1664]{1,0:T(8,128)(2,1)S(1)}, u32[]{:S(2)}) copy-start(bf16[16,1664]{1,0:T(8,128)(2,1)S(1)} %reshape.99) | copy-start | bytes 159748
  217.7 5.8 %copy-start.4 = (f32[7194,128]{1,0:T(8,128)S(1)}, f32[7194,128]{1,0:T(8,128)}, u32[]{:S(2)}) copy-start(f32[7194,128]{1,0:T(8,128)} %get-tuple-element.19) | copy-start | bytes 11049988
  223.5 3.4 %copy-start.3 = (f32[7194,128]{1,0:T(8,128)S(1)}, f32[7194,128]{1,0:T(8,128)}, u32[]{:S(2)}) copy-start(f32[7194,128]{1,0:T(8,128)} %get-tuple-element.20) | copy-start | bytes 11049988
  226.9 3.4 %copy-start.2 = (f32[7194,128]{1,0:T(8,128)S(1)}, f32[7194,128]{1,0:T(8,128)}, u32[]{:S(2)}) copy-start(f32[7194,128]{1,0:T(8,128)} %get-tuple-element.21) | copy-start | bytes 11049988

commit v2 on v1

v2 whole, which is shorter than its diff:
```python
import functools
import math
import jax
import jax.numpy as jnp
from jax import lax
from jax.experimental import pallas as pl
from jax.experimental.pallas import tpu as pltpu
from jax.sharding import PartitionSpec as P

MESH_AXES = ('outer', 'middle', 'inner')
ADAM_BETA1 = 0.9
ADAM_BETA2 = 0.98
ADAM_EPS = 1e-9
LEARN_RATE = 0.05
ADAM_STEP = 3

MESH = pl.DeviceIdType.MESH
F32 = jnp.float32
BF16 = jnp.bfloat16

LANES = 128
GROUP = 32
ROWS = 7366656 // LANES
SLICE_ROWS = ROWS // 8
CHUNKS = 19
CHUNK_GROUPS = 12
CHUNK = CHUNK_GROUPS * GROUP
HALF = CHUNK // 2
RING = 4
WINDOW = CHUNKS * CHUNK
LAST_ROWS = SLICE_ROWS - (CHUNKS - 1) * CHUNK
FRONT = 96
BOUNDS = (0, 1024, 1280, 1536, 1792, 1799)
PERMUTED = (1024, 1536)
START_MAX = BOUNDS[-1] - WINDOW // GROUP


def window_start(device):
    return min(SLICE_ROWS * device // GROUP, START_MAX)


def window_start_traced(device):
    return jnp.minimum(lax.div(device * SLICE_ROWS, GROUP), START_MAX)


def split_chunks():
    found = []
    for device in range(8):
        for chunk in range(CHUNKS):
            first = window_start(device) + chunk * CHUNK_GROUPS
            for tensor in range(4):
                edge = BOUNDS[tensor + 1]
                if first < edge < first + CHUNK_GROUPS:
                    found.append((first, tensor, edge - first))
    return tuple(found)


SPLITS = split_chunks()
FIRSTS = tuple(SLICE_ROWS * d // GROUP for d in range(8)) + (BOUNDS[-1] - 1,)


def step_kernel(e_ref, a_ref, f1_ref, f2_ref, b_ref, m_ref, v_ref, w_ref,
                m_out, v_out, w_out, wg_ref,
                acc, local, p1x, p1y, p2x, p2y, gflat, wflat, m_in,
                local_sem, d2d_send, d2d_recv, p1_send, p1x_recv, p1y_recv, p2_send, p2x_recv, p2y_recv,
                in_sem, ag_send, agx_recv, agy_recv, relay_send, relx_recv, rely_recv, fwd_send, fwd_recv):
    o, m, i = lax.axis_index('outer'), lax.axis_index('middle'), lax.axis_index('inner')
    x_dev, y_dev, p_dev = (o, 1 - m, i), (1 - o, m, i), (o, m, 1 - i)
    places = ((o, m), (o, 1 - m), (1 - o, m), (1 - o, 1 - m))
    mine = [(po * 2 + pm) * 2 + i for po, pm in places]
    theirs = [(po * 2 + pm) * 2 + (1 - i) for po, pm in places]
    start = window_start_traced(mine[0])
    shift = mine[0] * SLICE_ROWS - start * GROUP
    tensors = (e_ref, a_ref, f1_ref, f2_ref, b_ref)

    barrier = pltpu.get_barrier_semaphore()
    for device in (x_dev, y_dev, p_dev):
        pl.semaphore_signal(barrier, inc=1, device_id=device, device_id_type=MESH)
    pl.semaphore_wait(barrier, 3)

    def remote(src, dst, send, recv, device):
        pltpu.make_async_remote_copy(src_ref=src, dst_ref=dst, send_sem=send, recv_sem=recv, device_id=device, device_id_type=MESH).start()

    def drain(ref, sem):
        pltpu.make_async_copy(ref, ref, sem).wait()

    def load_chunk(device, chunk, copy):
        first = window_start_traced(device) + chunk * CHUNK_GROUPS
        for tensor in range(4):
            @pl.when((first >= BOUNDS[tensor]) & (first + CHUNK_GROUPS <= BOUNDS[tensor + 1]))
            def _():
                row = pl.multiple_of((first - BOUNDS[tensor]) * GROUP, GROUP)
                copy(tensors[tensor].at[pl.ds(row, CHUNK)], 0, CHUNK)
        for known, tensor, count in SPLITS:
            @pl.when(first == known)
            def _():
                head = count * GROUP
                copy(tensors[tensor].at[pl.ds((known - BOUNDS[tensor]) * GROUP, head)], 0, head)
                copy(tensors[tensor + 1].at[pl.ds(0, CHUNK - head)], head, CHUNK - head)

    def issue_gradients(chunk):
        slot = lax.rem(chunk, 3)
        base = pl.multiple_of(chunk * CHUNK, CHUNK)
        for j in (3, 1, 2, 0):
            load_chunk(theirs[j], chunk, lambda src, off, size: remote(
                src, acc.at[j, pl.ds(pl.multiple_of(base + off, GROUP), size)], d2d_send, d2d_recv.at[chunk], p_dev))
            load_chunk(mine[j], chunk, lambda src, off, size: pltpu.make_async_copy(
                src, local.at[slot, j, pl.ds(off, size)], local_sem.at[slot]).start())

    def add_rows(j, base, count, term):
        @pl.loop(0, count // GROUP)
        def _(r):
            off = pl.multiple_of(r * GROUP, GROUP)
            at = pl.ds(pl.multiple_of(base + off, GROUP), GROUP)
            acc[j, at] = acc[j, at] + term(off)

    def first_phase(chunk):
        slot = lax.rem(chunk, 3)
        ring = lax.rem(chunk, RING)
        base = pl.multiple_of(chunk * CHUNK, CHUNK)
        second = pl.multiple_of(base + HALF, HALF)
        drain(local.at[slot], local_sem.at[slot])
        drain(local.at[0], d2d_recv.at[chunk])
        add_rows(1, base, HALF, lambda off: local[slot, 1, pl.ds(off, GROUP)])
        add_rows(2, second, HALF, lambda off: local[slot, 2, pl.ds(HALF + off, GROUP)])
        add_rows(3, base, CHUNK, lambda off: local[slot, 3, pl.ds(off, GROUP)])
        remote(acc.at[1, pl.ds(base, HALF)], p1x.at[ring, 0], p1_send.at[0], p1x_recv.at[chunk], x_dev)
        remote(acc.at[2, pl.ds(second, HALF)], p1y.at[ring, 0], p1_send.at[1], p1y_recv.at[chunk], y_dev)
        remote(acc.at[3, pl.ds(base, HALF)], p1x.at[ring, 1], p1_send.at[0], p1x_recv.at[chunk], x_dev)
        remote(acc.at[3, pl.ds(second, HALF)], p1y.at[ring, 1], p1_send.at[1], p1y_recv.at[chunk], y_dev)
        add_rows(2, base, HALF, lambda off: local[slot, 2, pl.ds(off, GROUP)])
        add_rows(1, second, HALF, lambda off: local[slot, 1, pl.ds(HALF + off, GROUP)])
        add_rows(0, base, CHUNK, lambda off: local[slot, 0, pl.ds(off, GROUP)])

    def second_phase(chunk):
        ring = lax.rem(chunk, RING)
        base = pl.multiple_of(chunk * CHUNK, CHUNK)
        second = pl.multiple_of(base + HALF, HALF)
        drain(p1x.at[ring], p1x_recv.at[chunk])
        add_rows(2, base, HALF, lambda off: p1x[ring, 1, pl.ds(off, GROUP)])
        drain(p1y.at[ring], p1y_recv.at[chunk])
        add_rows(1, second, HALF, lambda off: p1y[ring, 1, pl.ds(off, GROUP)])
        remote(acc.at[2, pl.ds(base, HALF)], p2y.at[ring], p2_send.at[0], p2y_recv.at[chunk], y_dev)
        remote(acc.at[1, pl.ds(second, HALF)], p2x.at[ring], p2_send.at[1], p2x_recv.at[chunk], x_dev)
        add_rows(0, base, HALF, lambda off: p1x[ring, 0, pl.ds(off, GROUP)])
        add_rows(0, second, HALF, lambda off: p1y[ring, 0, pl.ds(off, GROUP)])

    def is_permuted(group):
        return (group >= PERMUTED[0]) & (group < PERMUTED[1])

    def last_phase(chunk):
        ring = lax.rem(chunk, RING)
        base = pl.multiple_of(chunk * CHUNK, CHUNK)
        first = start + chunk * CHUNK_GROUPS
        for part, (arrived, sem) in enumerate(((p2y, p2y_recv), (p2x, p2x_recv))):
            drain(arrived.at[ring], sem.at[chunk])

            @pl.loop(0, HALF // GROUP)
            def _(r):
                off = pl.multiple_of(r * GROUP, GROUP)
                row = pl.multiple_of(base + part * HALF + off, GROUP)
                total = acc[0, pl.ds(row, GROUP)] + arrived[ring, pl.ds(off, GROUP)]
                permuted = is_permuted(first + part * (HALF // GROUP) + r)

                @pl.when(permuted)
                def _():
                    for tile in range(4):
                        gflat[pl.ds(row + tile, 8, stride=4)] = total[8 * tile:8 * tile + 8]

                @pl.when(jnp.logical_not(permuted))
                def _():
                    gflat[pl.ds(row, GROUP)] = total

    def state_loads(block, size):
        slot = lax.rem(block, 2)
        at = pl.ds(pl.multiple_of(block * CHUNK, CHUNK), size)
        return [pltpu.make_async_copy(ref.at[at], m_in.at[slot, q, pl.ds(0, size)], in_sem.at[slot, q])
                for q, ref in enumerate((m_ref, v_ref, w_ref))]

    def start_loads(block):
        for last, size in ((False, CHUNK), (True, LAST_ROWS)):
            @pl.when((block == CHUNKS - 1) == last)
            def _():
                for copy in state_loads(block, size):
                    copy.start()

    def wait_loads(block):
        for last, size in ((False, CHUNK), (True, LAST_ROWS)):
            @pl.when((block == CHUNKS - 1) == last)
            def _():
                for copy in state_loads(block, size):
                    copy.wait()

    def adam_rows(slot, base, off, count):
        at = pl.ds(off, count)
        grad = gflat[pl.ds(base + off + shift, count)] / 8
        m_val = ADAM_BETA1 * m_in[slot, 0, at] + (1.0 - ADAM_BETA1) * grad
        v_val = ADAM_BETA2 * m_in[slot, 1, at] + (1.0 - ADAM_BETA2) * (grad * grad)
        m_hat = m_val / (1.0 - ADAM_BETA1 ** ADAM_STEP)
        v_hat = v_val / (1.0 - ADAM_BETA2 ** ADAM_STEP)
        w_val = m_in[slot, 2, at] - LEARN_RATE * m_hat / (jnp.sqrt(v_hat) + ADAM_EPS)
        out = pl.ds(pl.multiple_of(base + off, GROUP), count)
        m_out[out] = m_val
        v_out[out] = v_val
        w_out[out] = w_val
        wflat[pl.ds(pl.multiple_of(FRONT + base + off, GROUP), count)] = w_val

    def adam(block):
        slot = lax.rem(block, 2)
        base = pl.multiple_of(block * CHUNK, CHUNK)
        wait_loads(block)

        @pl.loop(0, jnp.where(block == CHUNKS - 1, LAST_ROWS // GROUP, CHUNK_GROUPS))
        def _(r):
            adam_rows(slot, base, pl.multiple_of(r * GROUP, GROUP), GROUP)

        @pl.when(block == CHUNKS - 1)
        def _():
            adam_rows((CHUNKS - 1) % 2, (CHUNKS - 1) * CHUNK, LAST_ROWS // GROUP * GROUP, LAST_ROWS % GROUP)

        @pl.loop(0, CHUNK_GROUPS)
        def _(r):
            row = pl.multiple_of(base + r * GROUP, GROUP)
            source = FRONT + row - shift
            permuted = is_permuted(start + block * CHUNK_GROUPS + r)

            @pl.when(permuted)
            def _():
                tiles = [wflat[pl.ds(source + tile, 8, stride=4)] for tile in range(4)]
                wg_ref[mine[0], pl.ds(row, GROUP)] = jnp.concatenate(tiles, axis=0).astype(BF16)

            @pl.when(jnp.logical_not(permuted))
            def _():
                wg_ref[mine[0], pl.ds(row, GROUP)] = wflat[pl.ds(source, GROUP)].astype(BF16)

        ours = wg_ref.at[mine[0], pl.ds(base, CHUNK)]
        remote(ours, ours, ag_send.at[0], agx_recv.at[block], x_dev)
        remote(ours, ours, ag_send.at[1], agy_recv.at[block], y_dev)
        remote(ours, ours, fwd_send.at[0], fwd_recv.at[0], p_dev)

    def relay(chunk):
        base = pl.multiple_of(chunk * CHUNK, CHUNK)
        at, head, tail = pl.ds(base, CHUNK), pl.ds(base, HALF), pl.ds(pl.multiple_of(base + HALF, HALF), HALF)
        drain(wg_ref.at[0, pl.ds(0, CHUNK)], agx_recv.at[chunk])
        remote(wg_ref.at[mine[1], head], wg_ref.at[mine[1], head], relay_send.at[0], rely_recv.at[chunk], y_dev)
        remote(wg_ref.at[mine[1], at], wg_ref.at[mine[1], at], fwd_send.at[1], fwd_recv.at[1], p_dev)
        drain(wg_ref.at[0, pl.ds(0, CHUNK)], agy_recv.at[chunk])
        remote(wg_ref.at[mine[2], tail], wg_ref.at[mine[2], tail], relay_send.at[1], relx_recv.at[chunk], x_dev)
        remote(wg_ref.at[mine[2], at], wg_ref.at[mine[2], at], fwd_send.at[2], fwd_recv.at[2], p_dev)

    def forward(chunk):
        base = pl.multiple_of(chunk * CHUNK, CHUNK)
        at = pl.ds(base, CHUNK)
        drain(wg_ref.at[0, pl.ds(0, HALF)], rely_recv.at[chunk])
        drain(wg_ref.at[0, pl.ds(0, HALF)], relx_recv.at[chunk])
        remote(wg_ref.at[mine[3], at], wg_ref.at[mine[3], at], fwd_send.at[3], fwd_recv.at[3], p_dev)

    issue_gradients(0)
    issue_gradients(1)

    stages = ((0, first_phase), (1, second_phase), (2, last_phase), (3, adam), (5, relay), (6, forward))

    @pl.loop(0, CHUNKS + stages[-1][0])
    def _(t):
        @pl.when(t + 2 < CHUNKS)
        def _():
            issue_gradients(t + 2)

        @pl.when((t >= 2) & (t - 2 < CHUNKS))
        def _():
            start_loads(t - 2)

        for lag, stage in stages:
            @pl.when((t >= lag) & (t - lag < CHUNKS))
            def _():
                stage(t - lag)

    drain(acc, d2d_send)
    for q in range(2):
        drain(acc.at[0], p1_send.at[q])
        drain(acc.at[0, pl.ds(0, WINDOW // 2)], p2_send.at[q])
        drain(wg_ref.at[0, pl.ds(0, WINDOW // 2)], relay_send.at[q])
        drain(wg_ref.at[0], ag_send.at[q])
    for q in range(4):
        drain(wg_ref.at[0], fwd_send.at[q])
        drain(wg_ref.at[0], fwd_recv.at[q])

    for d in range(1, 8):
        keep = SLICE_ROWS * d - FIRSTS[d] * GROUP
        row = lax.broadcasted_iota(jnp.int32, (GROUP, LANES), 0)
        if PERMUTED[0] <= FIRSTS[d] < PERMUTED[1]:
            row = 4 * (row % 8) + row // 8
        before = pl.ds((FIRSTS[d] - window_start(d - 1)) * GROUP, GROUP)
        after = pl.ds((FIRSTS[d] - window_start(d)) * GROUP, GROUP)
        wg_ref[d - 1, before] = jnp.where(row < keep, wg_ref[d - 1, before].astype(F32), wg_ref[d, after].astype(F32)).astype(BF16)


def step_call(tensors, state):
    hbm = pl.BlockSpec(memory_space=pl.ANY)
    dma = pltpu.SemaphoreType.DMA
    flat = pltpu.VMEM((SLICE_ROWS, LANES), F32)
    return pl.pallas_call(
        step_kernel,
        name='adam_step',
        out_shape=(flat, flat, flat, pltpu.VMEM((8, WINDOW, LANES), BF16)),
        in_specs=[hbm] * 8,
        out_specs=[pl.BlockSpec(memory_space=pltpu.VMEM)] * 4,
        scratch_shapes=[
            pltpu.VMEM((4, WINDOW, LANES), F32),
            pltpu.VMEM((3, 4, CHUNK, LANES), F32),
            pltpu.VMEM((RING, 2, HALF, LANES), F32),
            pltpu.VMEM((RING, 2, HALF, LANES), F32),
            pltpu.VMEM((RING, HALF, LANES), F32),
            pltpu.VMEM((RING, HALF, LANES), F32),
            pltpu.VMEM((WINDOW + 128, LANES), F32),
            pltpu.VMEM((WINDOW + FRONT, LANES), F32),
            pltpu.VMEM((2, 3, CHUNK, LANES), F32),
            dma((3,)), dma, dma((CHUNKS,)), dma((2,)), dma((CHUNKS,)), dma((CHUNKS,)), dma((2,)), dma((CHUNKS,)), dma((CHUNKS,)),
            dma((2, 3)), dma((2,)), dma((CHUNKS,)), dma((CHUNKS,)), dma((2,)), dma((CHUNKS,)), dma((CHUNKS,)),
            dma((4,)), dma((4,)),
        ],
        compiler_params=pltpu.CompilerParams(collective_id=0, has_side_effects=True, vmem_limit_bytes=32 * 1024 * 1024),
    )(*tensors, *state)


LAYERS = 16
PAIR_ROWS = 8192 + 3 * 2048 + 52
PAIR_SIZE = PAIR_ROWS * LANES
PARTS = 4


def place_kernel(mv_ref, vv_ref, wv_ref, wg_ref, m_out, v_out, w_out, e_ref, a_ref, f1_ref, f2_ref, b_ref, pair_ref, flat, wide, state_sem, out_sem, pair_sem):
    pair = lax.axis_index('outer') * 2 + lax.axis_index('middle')
    copies = []

    def put(src, dst, sem):
        copies.append(pltpu.make_async_copy(src, dst, sem))
        copies[-1].start()

    for q, (src, dst) in enumerate(((mv_ref, m_out), (vv_ref, v_out), (wv_ref, w_out))):
        put(src, dst, state_sem.at[q])
    count = 0
    for d in range(8):
        low, high = (FIRSTS[d] + 1 if d else 0), FIRSTS[d + 1] + 1
        for q, ref in enumerate((e_ref, a_ref, f1_ref, f2_ref, b_ref)):
            begin, end = max(low, BOUNDS[q]), min(high, BOUNDS[q + 1])
            if begin < end:
                offset = (begin - BOUNDS[q]) * GROUP
                size = min((end - begin) * GROUP, ref.shape[0] - offset)
                put(wg_ref.at[d, pl.ds((begin - window_start(d)) * GROUP, size)], ref.at[pl.ds(offset, size)], out_sem.at[count])
                count += 1

    def finish(begin, size, sem):
        put(flat.at[:, pl.ds(begin * LANES, size * LANES)], pair_ref.at[:, pl.ds(begin * LANES, size * LANES)], sem)

    def source(group, low, last, starts):
        late = group > last
        row = (group - jnp.where(late, starts[1], starts[0])) * GROUP
        return low + jnp.where(late, 1, 0), pl.multiple_of(row, GROUP)

    embed_starts = (window_start_traced(pair), window_start_traced(pair + 1))
    for part in range(PARTS):
        @pl.loop(part * 256 // PARTS, (part + 1) * 256 // PARTS)
        def _(g):
            d, row = source(pair * 256 + g, pair, embed_starts[1], embed_starts)
            for tile in range(4):
                flat[0:1, pl.ds(pl.multiple_of(g * 4096 + tile * 1024, 1024), 1024)] = wg_ref[d, pl.ds(row + 8 * tile, 8)].reshape(1, 1024)

        finish(part * 8192 // PARTS, 8192 // PARTS, pair_sem.at[part])

    for q in range(3):
        low = 4 + q
        base = 8192 + 2048 * q

        @pl.loop(0, LAYERS * 4)
        def _(g):
            d, row = source(BOUNDS[1 + q] + (g // 4) * 16 + pair * 4 + g % 4, low, FIRSTS[low + 1], (window_start(low), window_start(low + 1)))
            at = base * LANES + g * 4096
            if q < 2:
                group = wg_ref[d, pl.ds(row, GROUP)].astype(F32)
                for tile in range(4):
                    wide[g % 4, pl.ds(tile, 8, stride=4)] = group[8 * tile:8 * tile + 8]
            for tile in range(4):
                if q < 2:
                    rows = wide[g % 4, pl.ds(8 * tile, 8)].reshape(1, 1024).astype(BF16)
                else:
                    rows = wg_ref[d, pl.ds(row + 8 * tile, 8)].reshape(1, 1024)
                flat[0:1, pl.ds(pl.multiple_of(at + tile * 1024, 1024), 1024)] = rows

        finish(base, 2048, pair_sem.at[PARTS + q])
    for copy in copies:
        copy.wait()


def place_call(m_new, v_new, w_new, gathered):
    hbm = pl.BlockSpec(memory_space=pl.ANY)
    dma = pltpu.SemaphoreType.DMA
    flat = jax.ShapeDtypeStruct((SLICE_ROWS, LANES), F32)
    return pl.pallas_call(
        place_kernel,
        name='place_weights',
        out_shape=(flat, flat, flat) + tuple(jax.ShapeDtypeStruct((size, LANES), BF16) for size in (32768, 8192, 8192, 8192, 208))
        + (jax.ShapeDtypeStruct((1, PAIR_SIZE), BF16),),
        in_specs=[pl.BlockSpec(memory_space=pltpu.VMEM)] * 4,
        out_specs=[hbm] * 9,
        scratch_shapes=[
            pltpu.VMEM((1, PAIR_SIZE), BF16),
            pltpu.VMEM((4, GROUP, LANES), F32),
            dma((3,)), dma((12,)), dma((PARTS + 3,)),
        ],
        compiler_params=pltpu.CompilerParams(vmem_limit_bytes=12 * 1024 * 1024),
    )(*(pltpu.with_memory_space_constraint(x, pltpu.VMEM) for x in (m_new, v_new, w_new, gathered)))


def to_tiles(tensor):
    return tensor.reshape(256, 8, 4, LANES).transpose(0, 2, 1, 3).reshape(8192, LANES)


def from_tiles(rows):
    return rows.reshape(256, 4, 8, LANES).transpose(0, 2, 1, 3).reshape(16, 128, 512)


def solution(mesh):
    def local_step(g_embed, g_attn, g_ffn_in, g_ffn_out, g_vec, m_shard, v_shard, w_shard):
        vec_rows = jnp.pad(g_vec.reshape(208, LANES), ((0, 16), (0, 0)))
        tensors = (g_embed.reshape(32768, LANES), to_tiles(g_attn), to_tiles(g_ffn_in), g_ffn_out.reshape(8192, LANES), vec_rows)
        state = [shard.reshape(SLICE_ROWS, LANES) for shard in (m_shard, v_shard, w_shard)]
        m_new, v_new, w_new, gathered = step_call(tensors, state)
        m_new, v_new, w_new, embed, attn, ffn_in, ffn_out, vec, w_pair = place_call(m_new, v_new, w_new, gathered)
        wb_vec = vec.reshape(16, 1664)
        pair = lax.axis_index('outer') * 2 + lax.axis_index('middle')
        vec_block = lax.dynamic_slice_in_dim(wb_vec, pair * 416, 416, axis=1).reshape(1, -1)
        w_pair = lax.dynamic_update_slice(w_pair, vec_block, (0, PAIR_SIZE - 6656))
        return (m_new.reshape(-1), v_new.reshape(-1), w_new.reshape(-1), embed, from_tiles(attn), from_tiles(ffn_in),
                ffn_out.reshape(16, 512, 128), wb_vec, w_pair)

    return jax.shard_map(local_step, mesh=mesh, in_specs=(P(MESH_AXES),) * 8, out_specs=(P(MESH_AXES),) * 3 + (P(),) * 5 + (P(MESH_AXES),), check_vma=False)
```

time: 233 us -> 211 us (0.906)
  local copies, waits for them, and re-layouts: 23.5 us -> 2.48 us
  Pallas kernels: 198 us -> 208 us
  other arithmetic: 9.61 us -> 0 us
    unnamed x15 -> x2, local copies, waits for them, and re-layouts: 15.9 us -> 0.01 us
    pallas_call x1, Pallas kernels: 6.75 us -> 16.4 us  [place_call(): pl.pallas_call(place_kernel, name='place_weights', out_shape=(flat, flat,...]
    concatenate x1 -> x0, other arithmetic: 9.61 us -> none  [local_step(): w_chip = jnp.concatenate([chip_rows.reshape(-1), vec_block])[None, :]]
    broadcast_in_dim x1 -> x0, local copies, waits for them, and re-layouts: 5.77 us -> none  [local_step(): w_chip = jnp.concatenate([chip_rows.reshape(-1), vec_block])[None, :]]
where the time goes in v2:
time: 211 us
  Pallas kernels  208 us (99%)
  local copies, waits for them, and re-layouts  2.48 us (1%)
    pallas_call x1, Pallas kernels, step_call(): pl.pallas_call(step_kernel, name='adam_step', out_shape=(flat, flat, flat...  192 us
    pallas_call x1, Pallas kernels, place_call(): pl.pallas_call(place_kernel, name='place_weights', out_shape=(flat, flat,...  16.4 us

profile of v2, /device:TPU:0, one launch (start us, length us, event | category | flops | bytes accessed | tf_op | source)
XLA Modules:
  0.0 211.2 jit_solution(5078882478215195238)
XLA Ops:
  0.6 0.9 reshape.84
  1.5 0.7 pad.4.b_ref
  2.2 191.6 %adam_step.1 = (f32[7194,128]{1,0:T(8,128)S(1)}, f32[7194,128]{1,0:T(8,128)S(1)}, f32[7194,128]{1,0:T(8,128)S(1)}, bf16[8,7296,128]{2,1,0:T(8,128)(2,1)S(1)}) custom-call(f32[32768,128]{1,0:T(8,128)} %bitcast.29, f32[8192,128]{1,0:T(8,128)} %bitcast.30, f32[8192,128]{1,0:T(8,128)} %bitcast.31, f32[8192,128]{1,0:T(8,128)} %bitcast.32, f32[224,128]{1,0:T(8,128)} %pad.4.b_ref, ...), custom_call_target="tpu_custom_call" | custom-call | tf_op jit(solution)/shard_map/adam_step/pallas_call | solution.py:302
  193.8 16.4 %place_weights.1 = (f32[7194,128]{1,0:T(8,128)}, f32[7194,128]{1,0:T(8,128)}, f32[7194,128]{1,0:T(8,128)}, bf16[32768,128]{1,0:T(8,128)(2,1)}, bf16[8192,128]{1,...) custom-call(f32[7194,128]{1,0:T(8,128)S(1)} %get-tuple-element.22.mv, ...), custom_call_target="tpu_custom_call" | custom-call | tf_op jit(solution)/shard_map/place_weights/pallas_call | solution.py:399
  210.2 0.1 reshape.96
  210.3 0.0 copy-start
  210.4 0.1 constant_dynamic-slice_fusion
  210.4 0.1 reshape.97
  210.5 0.6 constant_dynamic-update-slice_fusion
  211.2 0.0 copy-done
Async XLA Ops:
  210.3 0.9 copy-start

commit v3 on v2

--- a/solution.py
+++ b/solution.py
@@ -360,32 +360,29 @@
 
     embed_starts = (window_start_traced(pair), window_start_traced(pair + 1))
     for part in range(PARTS):
-        @pl.loop(part * 256 // PARTS, (part + 1) * 256 // PARTS)
+        @pl.loop(part * 256 // PARTS, (part + 1) * 256 // PARTS, unroll=4)
         def _(g):
             d, row = source(pair * 256 + g, pair, embed_starts[1], embed_starts)
-            for tile in range(4):
-                flat[0:1, pl.ds(pl.multiple_of(g * 4096 + tile * 1024, 1024), 1024)] = wg_ref[d, pl.ds(row + 8 * tile, 8)].reshape(1, 1024)
+            flat[0:1, pl.ds(pl.multiple_of(g * 4096, 4096), 4096)] = wg_ref[d, pl.ds(row, GROUP)].reshape(1, 4096)
 
         finish(part * 8192 // PARTS, 8192 // PARTS, pair_sem.at[part])
 
-    for q in range(3):
+    for q in (2, 0, 1):
         low = 4 + q
         base = 8192 + 2048 * q
 
-        @pl.loop(0, LAYERS * 4)
-        def _(g):
-            d, row = source(BOUNDS[1 + q] + (g // 4) * 16 + pair * 4 + g % 4, low, FIRSTS[low + 1], (window_start(low), window_start(low + 1)))
-            at = base * LANES + g * 4096
-            if q < 2:
-                group = wg_ref[d, pl.ds(row, GROUP)].astype(F32)
-                for tile in range(4):
-                    wide[g % 4, pl.ds(tile, 8, stride=4)] = group[8 * tile:8 * tile + 8]
-            for tile in range(4):
+        @pl.loop(0, LAYERS, unroll=2)
+        def _(layer):
+            for g in range(4):
+                d, row = source(BOUNDS[1 + q] + layer * 16 + pair * 4 + g, low, FIRSTS[low + 1], (window_start(low), window_start(low + 1)))
+                group = wg_ref[d, pl.ds(row, GROUP)]
                 if q < 2:
-                    rows = wide[g % 4, pl.ds(8 * tile, 8)].reshape(1, 1024).astype(BF16)
-                else:
-                    rows = wg_ref[d, pl.ds(row + 8 * tile, 8)].reshape(1, 1024)
-                flat[0:1, pl.ds(pl.multiple_of(at + tile * 1024, 1024), 1024)] = rows
+                    turn = lax.rem(layer, 2)
+                    group = group.astype(F32)
+                    for tile in range(4):
+                        wide[turn, g, pl.ds(tile, 8, stride=4)] = group[8 * tile:8 * tile + 8]
+                    group = wide[turn, g].astype(BF16)
+                flat[0:1, pl.ds(pl.multiple_of((base + layer * 128 + g * GROUP) * LANES, 4096), 4096)] = group.reshape(1, 4096)
 
         finish(base, 2048, pair_sem.at[PARTS + q])
     for copy in copies:
@@ -405,7 +402,7 @@
         out_specs=[hbm] * 9,
         scratch_shapes=[
             pltpu.VMEM((1, PAIR_SIZE), BF16),
-            pltpu.VMEM((4, GROUP, LANES), F32),
+            pltpu.VMEM((2, 4, GROUP, LANES), F32),
             dma((3,)), dma((12,)), dma((PARTS + 3,)),
         ],
         compiler_params=pltpu.CompilerParams(vmem_limit_bytes=12 * 1024 * 1024),

time: 211 us -> 206 us (0.976)
  Pallas kernels: 208 us -> 203 us
    pallas_call x1, Pallas kernels: 16.4 us -> 11 us  [place_call(): pl.pallas_call(place_kernel, name='place_weights', out_shape=(flat, flat,...]
where the time goes in v3:
time: 206 us
  Pallas kernels  203 us (99%)
  local copies, waits for them, and re-layouts  2.48 us (1%)
    pallas_call x1, Pallas kernels, step_call(): pl.pallas_call(step_kernel, name='adam_step', out_shape=(flat, flat, flat...  192 us
    pallas_call x1, Pallas kernels, place_call(): pl.pallas_call(place_kernel, name='place_weights', out_shape=(flat, flat,...  11 us

profile of v3, /device:TPU:0, one launch (start us, length us, event | category | flops | bytes accessed | tf_op | source)
XLA Modules:
  0.0 205.7 jit_solution(3924826777753957731)
XLA Ops:
  0.6 0.9 reshape.84
  1.5 0.7 pad.4.b_ref
  2.2 191.6 %adam_step.1 = (f32[7194,128]{1,0:T(8,128)S(1)}, f32[7194,128]{1,0:T(8,128)S(1)}, f32[7194,128]{1,0:T(8,128)S(1)}, bf16[8,7296,128]{2,1,0:T(8,128)(2,1)S(1)}) custom-call(f32[32768,128]{1,0:T(8,128)} %bitcast.29, f32[8192,128]{1,0:T(8,128)} %bitcast.30, f32[8192,128]{1,0:T(8,128)} %bitcast.31, f32[8192,128]{1,0:T(8,128)} %bitcast.32, f32[224,128]{1,0:T(8,128)} %pad.4.b_ref, ...), custom_call_target="tpu_custom_call" | custom-call | tf_op jit(solution)/shard_map/adam_step/pallas_call | solution.py:302
  193.8 11.0 %place_weights.1 = (f32[7194,128]{1,0:T(8,128)}, f32[7194,128]{1,0:T(8,128)}, f32[7194,128]{1,0:T(8,128)}, bf16[32768,128]{1,0:T(8,128)(2,1)}, bf16[8192,128]{1,...) custom-call(f32[7194,128]{1,0:T(8,128)S(1)} %get-tuple-element.22.mv, ...), custom_call_target="tpu_custom_call" | custom-call | tf_op jit(solution)/shard_map/place_weights/pallas_call | solution.py:396
  204.8 0.1 reshape.96
  204.9 0.0 copy-start
  204.9 0.1 constant_dynamic-slice_fusion
  205.0 0.1 reshape.97
  205.1 0.6 constant_dynamic-update-slice_fusion
  205.7 0.0 copy-done
Async XLA Ops:
  204.9 0.9 copy-start

commit v4 on v3

v4 whole, which is shorter than its diff:
```python
import functools
import math
import jax
import jax.numpy as jnp
from jax import lax
from jax.experimental import pallas as pl
from jax.experimental.pallas import tpu as pltpu
from jax.sharding import PartitionSpec as P

MESH_AXES = ('outer', 'middle', 'inner')
ADAM_BETA1 = 0.9
ADAM_BETA2 = 0.98
ADAM_EPS = 1e-9
LEARN_RATE = 0.05
ADAM_STEP = 3

MESH = pl.DeviceIdType.MESH
F32 = jnp.float32
BF16 = jnp.bfloat16

LANES = 128
GROUP = 32
ROWS = 7366656 // LANES
SLICE_ROWS = ROWS // 8
CHUNK_GROUPS = 12
CHUNK = CHUNK_GROUPS * GROUP
HALF = CHUNK // 2
MAIN = 18
LAST = (6, 4)
CHUNKS = MAIN + len(LAST)
RING = 4
WINDOW_GROUPS = MAIN * CHUNK_GROUPS + sum(LAST)
WINDOW = WINDOW_GROUPS * GROUP
MARGIN = GROUP
BOUNDS = (0, 1024, 1280, 1536, 1792, 1799)
PERMUTED = (1024, 1536)
VEC_ROWS = 208
VEC_AT = (BOUNDS[4] - SLICE_ROWS * 7 // GROUP) * GROUP


def window_start(device):
    return SLICE_ROWS * device // GROUP


def window_start_traced(device):
    return lax.div(device * SLICE_ROWS, GROUP)


def chunk_groups(chunk):
    return CHUNK_GROUPS if chunk < MAIN else LAST[chunk - MAIN]


def chunk_first(chunk):
    return chunk * CHUNK_GROUPS if chunk <= MAIN else MAIN * CHUNK_GROUPS + sum(LAST[:chunk - MAIN])


def pieces(first, groups):
    found = []
    for tensor in range(5):
        low, high = max(first, BOUNDS[tensor]), min(first + groups, BOUNDS[tensor + 1])
        if low < high:
            row, off, size = (low - BOUNDS[tensor]) * GROUP, (low - first) * GROUP, (high - low) * GROUP
            if tensor == 4 and row + size > VEC_ROWS:
                found.append((tensor, 0, off + VEC_ROWS - row, row + size - VEC_ROWS))
                size = VEC_ROWS - row
            found.append((tensor, row, off, size))
    return tuple(found)


def split_chunks(groups):
    spans = [window_start(d) + chunk_first(c) for d in range(8) for c in range(CHUNKS) if chunk_groups(c) == groups]
    return [(first, pieces(first, groups)) for first in spans if len(pieces(first, groups)) > 1 or first >= BOUNDS[4]]


FIRSTS = tuple(SLICE_ROWS * d // GROUP for d in range(8)) + (BOUNDS[-1] - 1,)


def step_kernel(e_ref, a_ref, f1_ref, f2_ref, b_ref, m_ref, v_ref, w_ref,
                m_out, v_out, w_out, wg_ref,
                acc, local, p1x, p1y, p2x, p2y, gflat, wflat, m_in, stage, vec,
                stage_sem, local_sem, d2d_send, d2d_recv, p1_send, p1x_recv, p1y_recv, p2_send, p2x_recv, p2y_recv,
                in_sem, ag_send, agx_recv, agy_recv, relay_send, relx_recv, rely_recv, fwd_send, fwd_recv):
    o, m, i = lax.axis_index('outer'), lax.axis_index('middle'), lax.axis_index('inner')
    x_dev, y_dev, p_dev = (o, 1 - m, i), (1 - o, m, i), (o, m, 1 - i)
    places = ((o, m), (o, 1 - m), (1 - o, m), (1 - o, 1 - m))
    mine = [(po * 2 + pm) * 2 + i for po, pm in places]
    theirs = [(po * 2 + pm) * 2 + (1 - i) for po, pm in places]
    start = window_start_traced(mine[0])
    shift = mine[0] * SLICE_ROWS - start * GROUP
    tensors = (e_ref, a_ref, f1_ref, f2_ref, b_ref)

    barrier = pltpu.get_barrier_semaphore()
    for device in (x_dev, y_dev, p_dev):
        pl.semaphore_signal(barrier, inc=1, device_id=device, device_id_type=MESH)

    def remote(src, dst, send, recv, device):
        pltpu.make_async_remote_copy(src_ref=src, dst_ref=dst, send_sem=send, recv_sem=recv, device_id=device, device_id_type=MESH).start()

    def drain(ref, sem):
        pltpu.make_async_copy(ref, ref, sem).wait()

    def mod(value, base):
        return value % base if isinstance(value, int) else lax.rem(value, base)

    def load_chunk(device, base, size, copy):
        groups = size // GROUP
        first = window_start_traced(device) + (base // GROUP if isinstance(base, int) else lax.div(base, GROUP))
        for tensor in range(4):
            @pl.when((first >= BOUNDS[tensor]) & (first + groups <= BOUNDS[tensor + 1]))
            def _():
                row = pl.multiple_of((first - BOUNDS[tensor]) * GROUP, GROUP)
                copy(tensors[tensor].at[pl.ds(row, size)], 0, size)
        for known, parts in split_chunks(groups):
            @pl.when(first == known)
            def _():
                for tensor, row, off, count in parts:
                    copy(tensors[tensor].at[pl.ds(row, count)], off, count)

    def load_ours(j, chunk, base, size):
        slot = mod(chunk, 3)
        load_chunk(mine[j], base, size, lambda src, off, count: pltpu.make_async_copy(
            src, local.at[slot, j, pl.ds(off, count)], local_sem.at[slot, j]).start())

    def issue_gradients(chunk, base, size):
        for j in (3, 1, 2, 0):
            load_chunk(theirs[j], base, size, lambda src, off, count: remote(
                src, acc.at[j, pl.ds(pl.multiple_of(base + off, 8), count)], d2d_send, d2d_recv.at[chunk, j], p_dev))
            load_ours(j, chunk, base, size)

    def add_rows(j, base, count, term):
        @pl.loop(0, count // GROUP)
        def _(r):
            off = pl.multiple_of(r * GROUP, GROUP)
            at = pl.ds(pl.multiple_of(base + off, GROUP), GROUP)
            acc[j, at] = acc[j, at] + term(off)

    def middle(base, size):
        return base + size // 2 if isinstance(base, int) else pl.multiple_of(base + size // 2, GROUP)

    def first_phase(chunk, base, size):
        slot, ring = mod(chunk, 3), mod(chunk, RING)
        half, second = size // 2, middle(base, size)
        near = pl.ds(0, half)

        def ready(j):
            drain(local.at[0, 0, pl.ds(0, size)], local_sem.at[slot, j])
            drain(local.at[0, 0, pl.ds(0, size)], d2d_recv.at[chunk, j])

        ready(3)
        add_rows(3, base, size, lambda off: local[slot, 3, pl.ds(off, GROUP)])
        remote(acc.at[3, pl.ds(base, half)], p1x.at[ring, 1, near], p1_send.at[0], p1x_recv.at[chunk], x_dev)
        remote(acc.at[3, pl.ds(second, half)], p1y.at[ring, 1, near], p1_send.at[1], p1y_recv.at[chunk], y_dev)
        ready(1)
        add_rows(1, base, half, lambda off: local[slot, 1, pl.ds(off, GROUP)])
        remote(acc.at[1, pl.ds(base, half)], p1x.at[ring, 0, near], p1_send.at[0], p1x_recv.at[chunk], x_dev)
        ready(2)
        add_rows(2, second, half, lambda off: local[slot, 2, pl.ds(half + off, GROUP)])
        remote(acc.at[2, pl.ds(second, half)], p1y.at[ring, 0, near], p1_send.at[1], p1y_recv.at[chunk], y_dev)
        add_rows(1, second, half, lambda off: local[slot, 1, pl.ds(half + off, GROUP)])
        add_rows(2, base, half, lambda off: local[slot, 2, pl.ds(off, GROUP)])
        ready(0)
        add_rows(0, base, size, lambda off: local[slot, 0, pl.ds(off, GROUP)])

    def second_phase(chunk, base, size):
        ring = mod(chunk, RING)
        half, second = size // 2, middle(base, size)
        near = pl.ds(0, half)
        drain(local.at[0, 0, pl.ds(0, size)], p1x_recv.at[chunk])
        add_rows(2, base, half, lambda off: p1x[ring, 1, pl.ds(off, GROUP)])
        drain(local.at[0, 0, pl.ds(0, size)], p1y_recv.at[chunk])
        add_rows(1, second, half, lambda off: p1y[ring, 1, pl.ds(off, GROUP)])
        remote(acc.at[2, pl.ds(base, half)], p2y.at[ring, near], p2_send.at[0], p2y_recv.at[chunk], y_dev)
        remote(acc.at[1, pl.ds(second, half)], p2x.at[ring, near], p2_send.at[1], p2x_recv.at[chunk], x_dev)
        add_rows(0, base, half, lambda off: p1x[ring, 0, pl.ds(off, GROUP)])
        add_rows(0, second, half, lambda off: p1y[ring, 0, pl.ds(off, GROUP)])

    def is_permuted(group):
        return (group >= PERMUTED[0]) & (group < PERMUTED[1])

    def last_phase(chunk, base, size):
        ring = mod(chunk, RING)
        half = size // 2
        first = start + (base // GROUP if isinstance(base, int) else lax.div(base, GROUP))
        for part, (arrived, sem) in enumerate(((p2y, p2y_recv), (p2x, p2x_recv))):
            drain(local.at[0, 0, pl.ds(0, half)], sem.at[chunk])

            @pl.loop(0, half // GROUP)
            def _(r):
                off = pl.multiple_of(r * GROUP, GROUP)
                row = pl.multiple_of(base + part * half + off, GROUP)
                total = acc[0, pl.ds(row, GROUP)] + arrived[ring, pl.ds(off, GROUP)]
                permuted = is_permuted(first + part * (half // GROUP) + r)

                @pl.when(permuted)
                def _():
                    for tile in range(4):
                        gflat[pl.ds(row + tile, 8, stride=4)] = total[8 * tile:8 * tile + 8]

                @pl.when(jnp.logical_not(permuted))
                def _():
                    gflat[pl.ds(row, GROUP)] = total

        if isinstance(chunk, int) and chunk == CHUNKS - 1:
            @pl.when(mine[0] == 7)
            def _():
                vec[...] = gflat[pl.ds(VEC_AT, VEC_ROWS)]
                for tile in range(26):
                    gflat[pl.ds(VEC_AT + tile // 13 * 104 + tile % 13, 8, stride=13)] = vec[8 * tile:8 * tile + 8]

    def state_loads(block, base, size):
        slot = mod(block, 2)
        count = size if not isinstance(base, int) else min(size, SLICE_ROWS - base)
        at = pl.ds(base, count)
        return [pltpu.make_async_copy(ref.at[at], m_in.at[slot, q, pl.ds(0, count)], in_sem.at[slot, q])
                for q, ref in enumerate((m_ref, v_ref, w_ref))]

    def start_loads(block, base, size):
        for copy in state_loads(block, base, size):
            copy.start()

    def adam_rows(slot, base, off, count):
        at = pl.ds(off, count)
        grad = gflat[pl.ds(base + off + shift, count)] / 8
        m_val = ADAM_BETA1 * m_in[slot, 0, at] + (1.0 - ADAM_BETA1) * grad
        v_val = ADAM_BETA2 * m_in[slot, 1, at] + (1.0 - ADAM_BETA2) * (grad * grad)
        m_hat = m_val / (1.0 - ADAM_BETA1 ** ADAM_STEP)
        v_hat = v_val / (1.0 - ADAM_BETA2 ** ADAM_STEP)
        w_val = m_in[slot, 2, at] - LEARN_RATE * m_hat / (jnp.sqrt(v_hat) + ADAM_EPS)
        out = pl.ds(pl.multiple_of(base + off, GROUP), count)
        m_out[out] = m_val
        v_out[out] = v_val
        w_out[out] = w_val
        wflat[pl.ds(pl.multiple_of(MARGIN + base + off, GROUP), count)] = w_val

    def adam(block, base, size):
        slot = mod(block, 2)
        rows = size if not isinstance(base, int) else min(size, SLICE_ROWS - base)
        for copy in state_loads(block, base, size):
            copy.wait()

        @pl.loop(0, rows // GROUP)
        def _(r):
            adam_rows(slot, base, pl.multiple_of(r * GROUP, GROUP), GROUP)

        if rows % GROUP:
            adam_rows(slot, base, rows // GROUP * GROUP, rows % GROUP)
        first = start + (base // GROUP if isinstance(base, int) else lax.div(base, GROUP))

        @pl.loop(0, size // GROUP)
        def _(r):
            row = pl.multiple_of(base + r * GROUP, GROUP)
            source = MARGIN + row - shift
            permuted = is_permuted(first + r)

            @pl.when(permuted)
            def _():
                tiles = [wflat[pl.ds(source + tile, 8, stride=4)] for tile in range(4)]
                wg_ref[mine[0], pl.ds(row, GROUP)] = jnp.concatenate(tiles, axis=0).astype(BF16)

            @pl.when(jnp.logical_not(permuted))
            def _():
                wg_ref[mine[0], pl.ds(row, GROUP)] = wflat[pl.ds(source, GROUP)].astype(BF16)

        if isinstance(base, int) and base + size > VEC_AT:
            @pl.when(mine[0] == 7)
            def _():
                for pair in range(13):
                    row = VEC_AT + 16 * pair
                    if base <= row < base + size:
                        tiles = [wflat[pl.ds(MARGIN + VEC_AT - shift + tile // 13 * 104 + tile % 13, 8, stride=13)] for tile in (2 * pair, 2 * pair + 1)]
                        wg_ref[7, pl.ds(row, 16)] = jnp.concatenate(tiles, axis=0).astype(BF16)

        ours = wg_ref.at[mine[0], pl.ds(base, size)]
        remote(ours, ours, ag_send.at[0], agx_recv.at[block], x_dev)
        remote(ours, ours, ag_send.at[1], agy_recv.at[block], y_dev)
        remote(ours, ours, fwd_send.at[0], fwd_recv.at[0], p_dev)

    def relay(chunk, base, size):
        half = size // 2
        at, head, tail = pl.ds(base, size), pl.ds(base, half), pl.ds(middle(base, size), half)
        drain(wg_ref.at[0, pl.ds(0, size)], agx_recv.at[chunk])
        remote(wg_ref.at[mine[1], head], wg_ref.at[mine[1], head], relay_send.at[0], rely_recv.at[chunk], y_dev)
        remote(wg_ref.at[mine[1], at], wg_ref.at[mine[1], at], fwd_send.at[1], fwd_recv.at[1], p_dev)
        drain(wg_ref.at[0, pl.ds(0, size)], agy_recv.at[chunk])
        remote(wg_ref.at[mine[2], tail], wg_ref.at[mine[2], tail], relay_send.at[1], relx_recv.at[chunk], x_dev)
        remote(wg_ref.at[mine[2], at], wg_ref.at[mine[2], at], fwd_send.at[2], fwd_recv.at[2], p_dev)

    def forward(chunk, base, size):
        half = size // 2
        at = pl.ds(base, size)
        drain(wg_ref.at[0, pl.ds(0, half)], rely_recv.at[chunk])
        drain(wg_ref.at[0, pl.ds(0, half)], relx_recv.at[chunk])
        remote(wg_ref.at[mine[3], at], wg_ref.at[mine[3], at], fwd_send.at[3], fwd_recv.at[3], p_dev)

    for j in (3, 1, 2, 0):
        load_chunk(theirs[j], 0, CHUNK, lambda src, off, count: pltpu.make_async_copy(
            src, stage.at[j, pl.ds(off, count)], stage_sem.at[j]).start())
        load_ours(j, 0, 0, CHUNK)
    pl.semaphore_wait(barrier, 3)
    for j in (3, 1, 2, 0):
        drain(stage.at[j], stage_sem.at[j])
        remote(stage.at[j], acc.at[j, pl.ds(0, CHUNK)], d2d_send, d2d_recv.at[0, j], p_dev)
    issue_gradients(1, CHUNK, CHUNK)

    def run(chunk, action):
        @pl.when((chunk >= 0) & (chunk < MAIN))
        def _():
            action(chunk, pl.multiple_of(chunk * CHUNK, CHUNK), CHUNK)

        for last in range(MAIN, CHUNKS):
            @pl.when(chunk == last)
            def _():
                action(last, chunk_first(last) * GROUP, chunk_groups(last) * GROUP)

    stages = ((-2, issue_gradients), (2, start_loads), (0, first_phase), (1, second_phase), (2, last_phase), (3, adam), (7, relay), (10, forward))

    @pl.loop(0, CHUNKS + stages[-1][0])
    def _(t):
        for lag, action in stages:
            run(t - lag, action)

    drain(acc, d2d_send)
    for q in range(2):
        drain(acc.at[0], p1_send.at[q])
        drain(acc.at[0, pl.ds(0, WINDOW // 2)], p2_send.at[q])
        drain(wg_ref.at[0, pl.ds(0, WINDOW // 2)], relay_send.at[q])
        drain(wg_ref.at[0], ag_send.at[q])
    for q in range(4):
        drain(wg_ref.at[0], fwd_send.at[q])
        drain(wg_ref.at[0], fwd_recv.at[q])

    for d in range(1, 8):
        keep = SLICE_ROWS * d - FIRSTS[d] * GROUP
        row = lax.broadcasted_iota(jnp.int32, (GROUP, LANES), 0)
        if PERMUTED[0] <= FIRSTS[d] < PERMUTED[1]:
            row = 4 * (row % 8) + row // 8
        before = pl.ds((FIRSTS[d] - window_start(d - 1)) * GROUP, GROUP)
        after = pl.ds((FIRSTS[d] - window_start(d)) * GROUP, GROUP)
        wg_ref[d - 1, before] = jnp.where(row < keep, wg_ref[d - 1, before].astype(F32), wg_ref[d, after].astype(F32)).astype(BF16)


def step_call(tensors, state):
    hbm = pl.BlockSpec(memory_space=pl.ANY)
    dma = pltpu.SemaphoreType.DMA
    flat = pltpu.VMEM((SLICE_ROWS, LANES), F32)
    return pl.pallas_call(
        step_kernel,
        name='adam_step',
        out_shape=(flat, flat, flat, pltpu.VMEM((8, WINDOW, LANES), BF16)),
        in_specs=[hbm] * 8,
        out_specs=[pl.BlockSpec(memory_space=pltpu.VMEM)] * 4,
        scratch_shapes=[
            pltpu.VMEM((4, WINDOW, LANES), F32),
            pltpu.VMEM((3, 4, CHUNK, LANES), F32),
            pltpu.VMEM((RING, 2, HALF, LANES), F32),
            pltpu.VMEM((RING, 2, HALF, LANES), F32),
            pltpu.VMEM((RING, HALF, LANES), F32),
            pltpu.VMEM((RING, HALF, LANES), F32),
            pltpu.VMEM((WINDOW + MARGIN, LANES), F32),
            pltpu.VMEM((WINDOW + MARGIN, LANES), F32),
            pltpu.VMEM((2, 3, CHUNK, LANES), F32),
            pltpu.VMEM((4, CHUNK, LANES), F32),
            pltpu.VMEM((VEC_ROWS, LANES), F32),
            dma((4,)), dma((3, 4)), dma, dma((CHUNKS, 4)), dma((2,)), dma((CHUNKS,)), dma((CHUNKS,)), dma((2,)), dma((CHUNKS,)), dma((CHUNKS,)),
            dma((2, 3)), dma((2,)), dma((CHUNKS,)), dma((CHUNKS,)), dma((2,)), dma((CHUNKS,)), dma((CHUNKS,)),
            dma((4,)), dma((4,)),
        ],
        compiler_params=pltpu.CompilerParams(collective_id=0, has_side_effects=True, vmem_limit_bytes=32 * 1024 * 1024),
    )(*tensors, *state)


LAYERS = 16
PAIR_ROWS = 8192 + 3 * 2048 + 52
PAIR_SIZE = PAIR_ROWS * LANES
PARTS = 4


def place_kernel(mv_ref, vv_ref, wv_ref, wg_ref, m_out, v_out, w_out, e_ref, a_ref, f1_ref, f2_ref, b_ref, pair_ref, flat, wide, state_sem, out_sem, pair_sem):
    pair = lax.axis_index('outer') * 2 + lax.axis_index('middle')
    copies = []

    def put(src, dst, sem):
        copies.append(pltpu.make_async_copy(src, dst, sem))
        copies[-1].start()

    for q, (src, dst) in enumerate(((mv_ref, m_out), (vv_ref, v_out), (wv_ref, w_out))):
        put(src, dst, state_sem.at[q])
    count = 0
    for d in range(8):
        low, high = (FIRSTS[d] + 1 if d else 0), FIRSTS[d + 1] + 1
        for q, ref in enumerate((e_ref, a_ref, f1_ref, f2_ref, b_ref)):
            begin, end = max(low, BOUNDS[q]), min(high, BOUNDS[q + 1])
            if begin < end:
                offset = (begin - BOUNDS[q]) * GROUP
                size = min((end - begin) * GROUP, ref.shape[0] - offset)
                put(wg_ref.at[d, pl.ds((begin - window_start(d)) * GROUP, size)], ref.at[pl.ds(offset, size)], out_sem.at[count])
                count += 1

    def finish(begin, size, sem):
        put(flat.at[:, pl.ds(begin * LANES, size * LANES)], pair_ref.at[:, pl.ds(begin * LANES, size * LANES)], sem)

    def source(group, low, last, starts):
        late = group > last
        row = (group - jnp.where(late, starts[1], starts[0])) * GROUP
        return low + jnp.where(late, 1, 0), pl.multiple_of(row, GROUP)

    embed_starts = (window_start_traced(pair), window_start_traced(pair + 1))
    for part in range(PARTS):
        @pl.loop(part * 256 // PARTS, (part + 1) * 256 // PARTS, unroll=4)
        def _(g):
            d, row = source(pair * 256 + g, pair, embed_starts[1], embed_starts)
            flat[0:1, pl.ds(pl.multiple_of(g * 4096, 4096), 4096)] = wg_ref[d, pl.ds(row, GROUP)].reshape(1, 4096)

        finish(part * 8192 // PARTS, 8192 // PARTS, pair_sem.at[part])

    for q in (2, 0, 1):
        low = 4 + q
        base = 8192 + 2048 * q

        @pl.loop(0, LAYERS, unroll=2)
        def _(layer):
            for g in range(4):
                d, row = source(BOUNDS[1 + q] + layer * 16 + pair * 4 + g, low, FIRSTS[low + 1], (window_start(low), window_start(low + 1)))
                group = wg_ref[d, pl.ds(row, GROUP)]
                if q < 2:
                    turn = lax.rem(layer, 2)
                    group = group.astype(F32)
                    for tile in range(4):
                        wide[turn, g, pl.ds(tile, 8, stride=4)] = group[8 * tile:8 * tile + 8]
                    group = wide[turn, g].astype(BF16)
                flat[0:1, pl.ds(pl.multiple_of((base + layer * 128 + g * GROUP) * LANES, 4096), 4096)] = group.reshape(1, 4096)

        finish(base, 2048, pair_sem.at[PARTS + q])
    lines = []
    for half in range(2):
        tiles = [wg_ref[7, pl.ds(pl.multiple_of(VEC_AT + half * 104 + jnp.minimum(3 * pair + tile, 12) * 8, 8), 8)].astype(F32) for tile in range(5)]
        turned = pltpu.roll(jnp.concatenate(tiles, axis=1), 5 * LANES - 32 * pair, 1)
        lines += [turned[line:line + 1, :416] for line in range(8)]
    flat[0:1, pl.ds(14336 * LANES, 52 * LANES)] = jnp.concatenate(lines, axis=1).astype(BF16)
    finish(14336, 52, pair_sem.at[PARTS + 3])
    for copy in copies:
        copy.wait()


def place_call(m_new, v_new, w_new, gathered):
    hbm = pl.BlockSpec(memory_space=pl.ANY)
    dma = pltpu.SemaphoreType.DMA
    flat = jax.ShapeDtypeStruct((SLICE_ROWS, LANES), F32)
    return pl.pallas_call(
        place_kernel,
        name='place_weights',
        out_shape=(flat, flat, flat) + tuple(jax.ShapeDtypeStruct((size, LANES), BF16) for size in (32768, 8192, 8192, 8192, 208))
        + (jax.ShapeDtypeStruct((1, PAIR_SIZE), BF16),),
        in_specs=[pl.BlockSpec(memory_space=pltpu.VMEM)] * 4,
        out_specs=[hbm] * 9,
        scratch_shapes=[
            pltpu.VMEM((1, PAIR_SIZE), BF16),
            pltpu.VMEM((2, 4, GROUP, LANES), F32),
            dma((3,)), dma((12,)), dma((PARTS + 4,)),
        ],
        compiler_params=pltpu.CompilerParams(vmem_limit_bytes=12 * 1024 * 1024),
    )(*(pltpu.with_memory_space_constraint(x, pltpu.VMEM) for x in (m_new, v_new, w_new, gathered)))


def to_tiles(tensor):
    return tensor.reshape(256, 8, 4, LANES).transpose(0, 2, 1, 3).reshape(8192, LANES)


def from_tiles(rows):
    return rows.reshape(256, 4, 8, LANES).transpose(0, 2, 1, 3).reshape(16, 128, 512)


def solution(mesh):
    def local_step(g_embed, g_attn, g_ffn_in, g_ffn_out, g_vec, m_shard, v_shard, w_shard):
        vec_rows = g_vec.reshape(2, 8, 13, LANES).transpose(0, 2, 1, 3).reshape(VEC_ROWS, LANES)
        tensors = (g_embed.reshape(32768, LANES), to_tiles(g_attn), to_tiles(g_ffn_in), g_ffn_out.reshape(8192, LANES), vec_rows)
        state = [shard.reshape(SLICE_ROWS, LANES) for shard in (m_shard, v_shard, w_shard)]
        m_new, v_new, w_new, gathered = step_call(tensors, state)
        m_new, v_new, w_new, embed, attn, ffn_in, ffn_out, vec, w_pair = place_call(m_new, v_new, w_new, gathered)
        wb_vec = vec.reshape(2, 13, 8, LANES).transpose(0, 2, 1, 3).reshape(16, 1664)
        return (m_new.reshape(-1), v_new.reshape(-1), w_new.reshape(-1), embed, from_tiles(attn), from_tiles(ffn_in),
                ffn_out.reshape(16, 512, 128), wb_vec, w_pair)

    return jax.shard_map(local_step, mesh=mesh, in_specs=(P(MESH_AXES),) * 8, out_specs=(P(MESH_AXES),) * 3 + (P(),) * 5 + (P(MESH_AXES),), check_vma=False)
```

time: 206 us -> 201 us (0.976)
  Pallas kernels: 203 us -> 200 us
  local copies, waits for them, and re-layouts: 2.48 us -> 0 us
    pallas_call x1, Pallas kernels: 192 us -> 189 us  [step_call(): pl.pallas_call(step_kernel, name='adam_step', out_shape=(flat, flat, flat...]
where the time goes in v4:
time: 201 us
  Pallas kernels  200 us (100%)
    pallas_call x1, Pallas kernels, step_call(): pl.pallas_call(step_kernel, name='adam_step', out_shape=(flat, flat, flat...  189 us
    pallas_call x1, Pallas kernels, place_call(): pl.pallas_call(place_kernel, name='place_weights', out_shape=(flat, flat,...  11 us

profile of v4, /device:TPU:0, one launch (start us, length us, event | category | flops | bytes accessed | tf_op | source)
XLA Modules:
  0.0 200.5 jit_solution(12048398681665102157)
XLA Ops:
  0.6 188.9 %adam_step.1 = (f32[7194,128]{1,0:T(8,128)S(1)}, f32[7194,128]{1,0:T(8,128)S(1)}, f32[7194,128]{1,0:T(8,128)S(1)}, bf16[8,7232,128]{2,1,0:T(8,128)(2,1)S(1)}) custom-call(f32[32768,128]{1,0:T(8,128)} %bitcast.39, f32[8192,128]{1,0:T(8,128)} %bitcast.40, f32[8192,128]{1,0:T(8,128)} %bitcast.41, f32[8192,128]{1,0:T(8,128)} %bitcast.42, f32[208,128]{1,0:T(8,128)} %bitcast.46, ...), custom_call_target="tpu_custom_call" | custom-call | tf_op jit(solution)/shard_map/adam_step/pallas_call | solution.py:346
  189.6 11.0 %place_weights.1 = (f32[7194,128]{1,0:T(8,128)}, f32[7194,128]{1,0:T(8,128)}, f32[7194,128]{1,0:T(8,128)}, bf16[32768,128]{1,0:T(8,128)(2,1)}, bf16[8192,128]{1,...) custom-call(f32[7194,128]{1,0:T(8,128)S(1)} %get-tuple-element.22.mv, ...), custom_call_target="tpu_custom_call" | custom-call | tf_op jit(solution)/shard_map/place_weights/pallas_call | solution.py:449

commit v5 on v4

--- a/solution.py
+++ b/solution.py
@@ -22,14 +22,16 @@
 GROUP = 32
 ROWS = 7366656 // LANES
 SLICE_ROWS = ROWS // 8
-CHUNK_GROUPS = 12
+CHUNK_GROUPS = 24
 CHUNK = CHUNK_GROUPS * GROUP
 HALF = CHUNK // 2
-MAIN = 18
-LAST = (6, 4)
-CHUNKS = MAIN + len(LAST)
+LEAD = (4, 12)
+MAIN = 8
+LAST = (18,)
+SIZES = LEAD + (CHUNK_GROUPS,) * MAIN + LAST
+CHUNKS = len(SIZES)
 RING = 4
-WINDOW_GROUPS = MAIN * CHUNK_GROUPS + sum(LAST)
+WINDOW_GROUPS = sum(SIZES)
 WINDOW = WINDOW_GROUPS * GROUP
 MARGIN = GROUP
 BOUNDS = (0, 1024, 1280, 1536, 1792, 1799)
@@ -46,12 +48,8 @@
     return lax.div(device * SLICE_ROWS, GROUP)
 
 
-def chunk_groups(chunk):
-    return CHUNK_GROUPS if chunk < MAIN else LAST[chunk - MAIN]
-
-
 def chunk_first(chunk):
-    return chunk * CHUNK_GROUPS if chunk <= MAIN else MAIN * CHUNK_GROUPS + sum(LAST[:chunk - MAIN])
+    return sum(SIZES[:chunk])
 
 
 def pieces(first, groups):
@@ -68,7 +66,7 @@
 
 
 def split_chunks(groups):
-    spans = [window_start(d) + chunk_first(c) for d in range(8) for c in range(CHUNKS) if chunk_groups(c) == groups]
+    spans = [window_start(d) + chunk_first(c) for d in range(8) for c in range(CHUNKS) if SIZES[c] == groups]
     return [(first, pieces(first, groups)) for first in spans if len(pieces(first, groups)) > 1 or first >= BOUNDS[4]]
 
 
@@ -292,25 +290,28 @@
         drain(wg_ref.at[0, pl.ds(0, half)], relx_recv.at[chunk])
         remote(wg_ref.at[mine[3], at], wg_ref.at[mine[3], at], fwd_send.at[3], fwd_recv.at[3], p_dev)
 
+    begin = SIZES[0] * GROUP
     for j in (3, 1, 2, 0):
-        load_chunk(theirs[j], 0, CHUNK, lambda src, off, count: pltpu.make_async_copy(
+        load_chunk(theirs[j], 0, begin, lambda src, off, count: pltpu.make_async_copy(
             src, stage.at[j, pl.ds(off, count)], stage_sem.at[j]).start())
-        load_ours(j, 0, 0, CHUNK)
+        load_ours(j, 0, 0, begin)
     pl.semaphore_wait(barrier, 3)
     for j in (3, 1, 2, 0):
         drain(stage.at[j], stage_sem.at[j])
-        remote(stage.at[j], acc.at[j, pl.ds(0, CHUNK)], d2d_send, d2d_recv.at[0, j], p_dev)
-    issue_gradients(1, CHUNK, CHUNK)
+        remote(stage.at[j], acc.at[j, pl.ds(0, begin)], d2d_send, d2d_recv.at[0, j], p_dev)
+    issue_gradients(1, chunk_first(1) * GROUP, SIZES[1] * GROUP)
 
     def run(chunk, action):
-        @pl.when((chunk >= 0) & (chunk < MAIN))
+        lead = len(LEAD)
+
+        @pl.when((chunk >= lead) & (chunk < lead + MAIN))
         def _():
-            action(chunk, pl.multiple_of(chunk * CHUNK, CHUNK), CHUNK)
-
-        for last in range(MAIN, CHUNKS):
-            @pl.when(chunk == last)
-            def _():
-                action(last, chunk_first(last) * GROUP, chunk_groups(last) * GROUP)
+            action(chunk, pl.multiple_of(chunk * CHUNK + (sum(LEAD) - lead * CHUNK_GROUPS) * GROUP, GROUP), CHUNK)
+
+        for other in [*range(lead), *range(lead + MAIN, CHUNKS)]:
+            @pl.when(chunk == other)
+            def _():
+                action(other, chunk_first(other) * GROUP, SIZES[other] * GROUP)
 
     stages = ((-2, issue_gradients), (2, start_loads), (0, first_phase), (1, second_phase), (2, last_phase), (3, adam), (7, relay), (10, forward))
 
@@ -359,13 +360,13 @@
             pltpu.VMEM((WINDOW + MARGIN, LANES), F32),
             pltpu.VMEM((WINDOW + MARGIN, LANES), F32),
             pltpu.VMEM((2, 3, CHUNK, LANES), F32),
-            pltpu.VMEM((4, CHUNK, LANES), F32),
+            pltpu.VMEM((4, SIZES[0] * GROUP, LANES), F32),
             pltpu.VMEM((VEC_ROWS, LANES), F32),
             dma((4,)), dma((3, 4)), dma, dma((CHUNKS, 4)), dma((2,)), dma((CHUNKS,)), dma((CHUNKS,)), dma((2,)), dma((CHUNKS,)), dma((CHUNKS,)),
             dma((2, 3)), dma((2,)), dma((CHUNKS,)), dma((CHUNKS,)), dma((2,)), dma((CHUNKS,)), dma((CHUNKS,)),
             dma((4,)), dma((4,)),
         ],
-        compiler_params=pltpu.CompilerParams(collective_id=0, has_side_effects=True, vmem_limit_bytes=32 * 1024 * 1024),
+        compiler_params=pltpu.CompilerParams(collective_id=0, has_side_effects=True, vmem_limit_bytes=36 * 1024 * 1024),
     )(*tensors, *state)
 
 

time: 201 us -> 199 us (0.990)
  no operation moved by 1% of the time
where the time goes in v5:
time: 199 us
  Pallas kernels  199 us (100%)
    pallas_call x1, Pallas kernels, step_call(): pl.pallas_call(step_kernel, name='adam_step', out_shape=(flat, flat, flat...  188 us
    pallas_call x1, Pallas kernels, place_call(): pl.pallas_call(place_kernel, name='place_weights', out_shape=(flat, flat,...  11 us

profile of v5, /device:TPU:0, one launch (start us, length us, event | category | flops | bytes accessed | tf_op | source)
XLA Modules:
  0.0 199.2 jit_solution(7963644532666739771)
XLA Ops:
  0.6 187.6 %adam_step.1 = (f32[7194,128]{1,0:T(8,128)S(1)}, f32[7194,128]{1,0:T(8,128)S(1)}, f32[7194,128]{1,0:T(8,128)S(1)}, bf16[8,7232,128]{2,1,0:T(8,128)(2,1)S(1)}) custom-call(f32[32768,128]{1,0:T(8,128)} %bitcast.39, f32[8192,128]{1,0:T(8,128)} %bitcast.40, f32[8192,128]{1,0:T(8,128)} %bitcast.41, f32[8192,128]{1,0:T(8,128)} %bitcast.42, f32[208,128]{1,0:T(8,128)} %bitcast.46, ...), custom_call_target="tpu_custom_call" | custom-call | tf_op jit(solution)/shard_map/adam_step/pallas_call | solution.py:347
  188.2 11.0 %place_weights.1 = (f32[7194,128]{1,0:T(8,128)}, f32[7194,128]{1,0:T(8,128)}, f32[7194,128]{1,0:T(8,128)}, bf16[32768,128]{1,0:T(8,128)(2,1)}, bf16[8192,128]{1,...) custom-call(f32[7194,128]{1,0:T(8,128)S(1)} %get-tuple-element.22.mv, ...), custom_call_target="tpu_custom_call" | custom-call | tf_op jit(solution)/shard_map/place_weights/pallas_call | solution.py:450

commit v6 on v5

--- a/solution.py
+++ b/solution.py
@@ -13,6 +13,7 @@
 ADAM_EPS = 1e-9
 LEARN_RATE = 0.05
 ADAM_STEP = 3
+STEP_RATE = LEARN_RATE / (1.0 - ADAM_BETA1 ** ADAM_STEP)
 
 MESH = pl.DeviceIdType.MESH
 F32 = jnp.float32
@@ -221,9 +222,8 @@
         grad = gflat[pl.ds(base + off + shift, count)] / 8
         m_val = ADAM_BETA1 * m_in[slot, 0, at] + (1.0 - ADAM_BETA1) * grad
         v_val = ADAM_BETA2 * m_in[slot, 1, at] + (1.0 - ADAM_BETA2) * (grad * grad)
-        m_hat = m_val / (1.0 - ADAM_BETA1 ** ADAM_STEP)
         v_hat = v_val / (1.0 - ADAM_BETA2 ** ADAM_STEP)
-        w_val = m_in[slot, 2, at] - LEARN_RATE * m_hat / (jnp.sqrt(v_hat) + ADAM_EPS)
+        w_val = m_in[slot, 2, at] - STEP_RATE * m_val / (jnp.sqrt(v_hat) + ADAM_EPS)
         out = pl.ds(pl.multiple_of(base + off, GROUP), count)
         m_out[out] = m_val
         v_out[out] = v_val

time: 199 us -> 199 us (level)
  no operation moved by 1% of the time
where the time goes in v6:
time: 199 us
  Pallas kernels  199 us (100%)
    pallas_call x1, Pallas kernels, step_call(): pl.pallas_call(step_kernel, name='adam_step', out_shape=(flat, flat, flat...  188 us
    pallas_call x1, Pallas kernels, place_call(): pl.pallas_call(place_kernel, name='place_weights', out_shape=(flat, flat,...  11 us

profile of v6, /device:TPU:0, one launch (start us, length us, event | category | flops | bytes accessed | tf_op | source)
XLA Modules:
  0.0 199.2 jit_solution(921703888106722025)
XLA Ops:
  0.6 187.6 %adam_step.1 = (f32[7194,128]{1,0:T(8,128)S(1)}, f32[7194,128]{1,0:T(8,128)S(1)}, f32[7194,128]{1,0:T(8,128)S(1)}, bf16[8,7232,128]{2,1,0:T(8,128)(2,1)S(1)}) custom-call(f32[32768,128]{1,0:T(8,128)} %bitcast.39, f32[8192,128]{1,0:T(8,128)} %bitcast.40, f32[8192,128]{1,0:T(8,128)} %bitcast.41, f32[8192,128]{1,0:T(8,128)} %bitcast.42, f32[208,128]{1,0:T(8,128)} %bitcast.46, ...), custom_call_target="tpu_custom_call" | custom-call | tf_op jit(solution)/shard_map/adam_step/pallas_call | solution.py:347
  188.2 11.0 %place_weights.1 = (f32[7194,128]{1,0:T(8,128)}, f32[7194,128]{1,0:T(8,128)}, f32[7194,128]{1,0:T(8,128)}, bf16[32768,128]{1,0:T(8,128)(2,1)}, bf16[8192,128]{1,...) custom-call(f32[7194,128]{1,0:T(8,128)S(1)} %get-tuple-element.22.mv, ...), custom_call_target="tpu_custom_call" | custom-call | tf_op jit(solution)/shard_map/place_weights/pallas_call | solution.py:450

commit v7 on v6

--- a/solution.py
+++ b/solution.py
@@ -32,6 +32,8 @@
 SIZES = LEAD + (CHUNK_GROUPS,) * MAIN + LAST
 CHUNKS = len(SIZES)
 RING = 4
+D2D_RING = 6
+OUT_RING = 5
 WINDOW_GROUPS = sum(SIZES)
 WINDOW = WINDOW_GROUPS * GROUP
 MARGIN = GROUP
@@ -77,8 +79,7 @@
 def step_kernel(e_ref, a_ref, f1_ref, f2_ref, b_ref, m_ref, v_ref, w_ref,
                 m_out, v_out, w_out, wg_ref,
                 acc, local, p1x, p1y, p2x, p2y, gflat, wflat, m_in, stage, vec,
-                stage_sem, local_sem, d2d_send, d2d_recv, p1_send, p1x_recv, p1y_recv, p2_send, p2x_recv, p2y_recv,
-                in_sem, ag_send, agx_recv, agy_recv, relay_send, relx_recv, rely_recv, fwd_send, fwd_recv):
+                stage_sem, local_sem, d2d_send, d2d_recv, sum_send, p1_recv, p2_recv, in_sem, out_send, ag_recv, relay_recv, fwd_recv):
     o, m, i = lax.axis_index('outer'), lax.axis_index('middle'), lax.axis_index('inner')
     x_dev, y_dev, p_dev = (o, 1 - m, i), (1 - o, m, i), (o, m, 1 - i)
     places = ((o, m), (o, 1 - m), (1 - o, m), (1 - o, 1 - m))
@@ -118,12 +119,12 @@
     def load_ours(j, chunk, base, size):
         slot = mod(chunk, 3)
         load_chunk(mine[j], base, size, lambda src, off, count: pltpu.make_async_copy(
-            src, local.at[slot, j, pl.ds(off, count)], local_sem.at[slot, j]).start())
+            src, local.at[slot, j, pl.ds(off, count)], local_sem.at[slot, int(j != 3)]).start())
 
     def issue_gradients(chunk, base, size):
         for j in (3, 1, 2, 0):
             load_chunk(theirs[j], base, size, lambda src, off, count: remote(
-                src, acc.at[j, pl.ds(pl.multiple_of(base + off, 8), count)], d2d_send, d2d_recv.at[chunk, j], p_dev))
+                src, acc.at[j, pl.ds(pl.multiple_of(base + off, 8), count)], d2d_send, d2d_recv.at[mod(chunk, D2D_RING), int(j != 3)], p_dev))
             load_ours(j, chunk, base, size)
 
     def add_rows(j, base, count, term):
@@ -141,35 +142,33 @@
         half, second = size // 2, middle(base, size)
         near = pl.ds(0, half)
 
-        def ready(j):
-            drain(local.at[0, 0, pl.ds(0, size)], local_sem.at[slot, j])
-            drain(local.at[0, 0, pl.ds(0, size)], d2d_recv.at[chunk, j])
-
-        ready(3)
+        def ready(j, count):
+            arrived = local.at[0, pl.ds(0, count), pl.ds(0, size)]
+            drain(arrived, local_sem.at[slot, j])
+            drain(arrived, d2d_recv.at[mod(chunk, D2D_RING), j])
+
+        ready(0, 1)
         add_rows(3, base, size, lambda off: local[slot, 3, pl.ds(off, GROUP)])
-        remote(acc.at[3, pl.ds(base, half)], p1x.at[ring, 1, near], p1_send.at[0], p1x_recv.at[chunk], x_dev)
-        remote(acc.at[3, pl.ds(second, half)], p1y.at[ring, 1, near], p1_send.at[1], p1y_recv.at[chunk], y_dev)
-        ready(1)
+        remote(acc.at[3, pl.ds(base, half)], p1x.at[ring, 1, near], sum_send, p1_recv.at[ring], x_dev)
+        remote(acc.at[3, pl.ds(second, half)], p1y.at[ring, 1, near], sum_send, p1_recv.at[ring], y_dev)
+        ready(1, 3)
         add_rows(1, base, half, lambda off: local[slot, 1, pl.ds(off, GROUP)])
-        remote(acc.at[1, pl.ds(base, half)], p1x.at[ring, 0, near], p1_send.at[0], p1x_recv.at[chunk], x_dev)
-        ready(2)
+        remote(acc.at[1, pl.ds(base, half)], p1x.at[ring, 0, near], sum_send, p1_recv.at[ring], x_dev)
         add_rows(2, second, half, lambda off: local[slot, 2, pl.ds(half + off, GROUP)])
-        remote(acc.at[2, pl.ds(second, half)], p1y.at[ring, 0, near], p1_send.at[1], p1y_recv.at[chunk], y_dev)
+        remote(acc.at[2, pl.ds(second, half)], p1y.at[ring, 0, near], sum_send, p1_recv.at[ring], y_dev)
         add_rows(1, second, half, lambda off: local[slot, 1, pl.ds(half + off, GROUP)])
         add_rows(2, base, half, lambda off: local[slot, 2, pl.ds(off, GROUP)])
-        ready(0)
         add_rows(0, base, size, lambda off: local[slot, 0, pl.ds(off, GROUP)])
 
     def second_phase(chunk, base, size):
         ring = mod(chunk, RING)
         half, second = size // 2, middle(base, size)
         near = pl.ds(0, half)
-        drain(local.at[0, 0, pl.ds(0, size)], p1x_recv.at[chunk])
+        drain(local.at[0, pl.ds(0, 2), pl.ds(0, size)], p1_recv.at[ring])
         add_rows(2, base, half, lambda off: p1x[ring, 1, pl.ds(off, GROUP)])
-        drain(local.at[0, 0, pl.ds(0, size)], p1y_recv.at[chunk])
         add_rows(1, second, half, lambda off: p1y[ring, 1, pl.ds(off, GROUP)])
-        remote(acc.at[2, pl.ds(base, half)], p2y.at[ring, near], p2_send.at[0], p2y_recv.at[chunk], y_dev)
-        remote(acc.at[1, pl.ds(second, half)], p2x.at[ring, near], p2_send.at[1], p2x_recv.at[chunk], x_dev)
+        remote(acc.at[2, pl.ds(base, half)], p2y.at[ring, near], sum_send, p2_recv.at[ring], y_dev)
+        remote(acc.at[1, pl.ds(second, half)], p2x.at[ring, near], sum_send, p2_recv.at[ring], x_dev)
         add_rows(0, base, half, lambda off: p1x[ring, 0, pl.ds(off, GROUP)])
         add_rows(0, second, half, lambda off: p1y[ring, 0, pl.ds(off, GROUP)])
 
@@ -180,9 +179,8 @@
         ring = mod(chunk, RING)
         half = size // 2
         first = start + (base // GROUP if isinstance(base, int) else lax.div(base, GROUP))
-        for part, (arrived, sem) in enumerate(((p2y, p2y_recv), (p2x, p2x_recv))):
-            drain(local.at[0, 0, pl.ds(0, half)], sem.at[chunk])
-
+        drain(local.at[0, 0, pl.ds(0, size)], p2_recv.at[ring])
+        for part, arrived in enumerate((p2y, p2x)):
             @pl.loop(0, half // GROUP)
             def _(r):
                 off = pl.multiple_of(r * GROUP, GROUP)
@@ -206,16 +204,11 @@
                 for tile in range(26):
                     gflat[pl.ds(VEC_AT + tile // 13 * 104 + tile % 13, 8, stride=13)] = vec[8 * tile:8 * tile + 8]
 
-    def state_loads(block, base, size):
+    def start_loads(block, base, size):
         slot = mod(block, 2)
         count = size if not isinstance(base, int) else min(size, SLICE_ROWS - base)
-        at = pl.ds(base, count)
-        return [pltpu.make_async_copy(ref.at[at], m_in.at[slot, q, pl.ds(0, count)], in_sem.at[slot, q])
-                for q, ref in enumerate((m_ref, v_ref, w_ref))]
-
-    def start_loads(block, base, size):
-        for copy in state_loads(block, base, size):
-            copy.start()
+        for q, ref in enumerate((m_ref, v_ref, w_ref)):
+            pltpu.make_async_copy(ref.at[pl.ds(base, count)], m_in.at[slot, q, pl.ds(0, count)], in_sem.at[slot]).start()
 
     def adam_rows(slot, base, off, count):
         at = pl.ds(off, count)
@@ -233,8 +226,7 @@
     def adam(block, base, size):
         slot = mod(block, 2)
         rows = size if not isinstance(base, int) else min(size, SLICE_ROWS - base)
-        for copy in state_loads(block, base, size):
-            copy.wait()
+        drain(m_in.at[slot, :, pl.ds(0, rows)], in_sem.at[slot])
 
         @pl.loop(0, rows // GROUP)
         def _(r):
@@ -269,36 +261,36 @@
                         wg_ref[7, pl.ds(row, 16)] = jnp.concatenate(tiles, axis=0).astype(BF16)
 
         ours = wg_ref.at[mine[0], pl.ds(base, size)]
-        remote(ours, ours, ag_send.at[0], agx_recv.at[block], x_dev)
-        remote(ours, ours, ag_send.at[1], agy_recv.at[block], y_dev)
-        remote(ours, ours, fwd_send.at[0], fwd_recv.at[0], p_dev)
+        remote(ours, ours, out_send, ag_recv.at[mod(block, OUT_RING)], x_dev)
+        remote(ours, ours, out_send, ag_recv.at[mod(block, OUT_RING)], y_dev)
+        remote(ours, ours, out_send, fwd_recv, p_dev)
 
     def relay(chunk, base, size):
-        half = size // 2
+        half, turn = size // 2, mod(chunk, OUT_RING)
         at, head, tail = pl.ds(base, size), pl.ds(base, half), pl.ds(middle(base, size), half)
-        drain(wg_ref.at[0, pl.ds(0, size)], agx_recv.at[chunk])
-        remote(wg_ref.at[mine[1], head], wg_ref.at[mine[1], head], relay_send.at[0], rely_recv.at[chunk], y_dev)
-        remote(wg_ref.at[mine[1], at], wg_ref.at[mine[1], at], fwd_send.at[1], fwd_recv.at[1], p_dev)
-        drain(wg_ref.at[0, pl.ds(0, size)], agy_recv.at[chunk])
-        remote(wg_ref.at[mine[2], tail], wg_ref.at[mine[2], tail], relay_send.at[1], relx_recv.at[chunk], x_dev)
-        remote(wg_ref.at[mine[2], at], wg_ref.at[mine[2], at], fwd_send.at[2], fwd_recv.at[2], p_dev)
+        drain(wg_ref.at[pl.ds(0, 2), pl.ds(0, size)], ag_recv.at[turn])
+        remote(wg_ref.at[mine[1], head], wg_ref.at[mine[1], head], out_send, relay_recv.at[turn], y_dev)
+        remote(wg_ref.at[mine[2], tail], wg_ref.at[mine[2], tail], out_send, relay_recv.at[turn], x_dev)
+        remote(wg_ref.at[mine[1], at], wg_ref.at[mine[1], at], out_send, fwd_recv, p_dev)
+        remote(wg_ref.at[mine[2], at], wg_ref.at[mine[2], at], out_send, fwd_recv, p_dev)
 
     def forward(chunk, base, size):
-        half = size // 2
         at = pl.ds(base, size)
-        drain(wg_ref.at[0, pl.ds(0, half)], rely_recv.at[chunk])
-        drain(wg_ref.at[0, pl.ds(0, half)], relx_recv.at[chunk])
-        remote(wg_ref.at[mine[3], at], wg_ref.at[mine[3], at], fwd_send.at[3], fwd_recv.at[3], p_dev)
+        drain(wg_ref.at[0, pl.ds(0, size)], relay_recv.at[mod(chunk, OUT_RING)])
+        remote(wg_ref.at[mine[3], at], wg_ref.at[mine[3], at], out_send, fwd_recv, p_dev)
 
     begin = SIZES[0] * GROUP
     for j in (3, 1, 2, 0):
         load_chunk(theirs[j], 0, begin, lambda src, off, count: pltpu.make_async_copy(
-            src, stage.at[j, pl.ds(off, count)], stage_sem.at[j]).start())
+            src, stage.at[j, pl.ds(off, count)], stage_sem.at[int(j != 3)]).start())
         load_ours(j, 0, 0, begin)
     pl.semaphore_wait(barrier, 3)
     for j in (3, 1, 2, 0):
-        drain(stage.at[j], stage_sem.at[j])
-        remote(stage.at[j], acc.at[j, pl.ds(0, begin)], d2d_send, d2d_recv.at[0, j], p_dev)
+        if j == 3:
+            drain(stage.at[3], stage_sem.at[0])
+        elif j == 1:
+            drain(stage.at[pl.ds(0, 3)], stage_sem.at[1])
+        remote(stage.at[j], acc.at[j, pl.ds(0, begin)], d2d_send, d2d_recv.at[0, int(j != 3)], p_dev)
     issue_gradients(1, chunk_first(1) * GROUP, SIZES[1] * GROUP)
 
     def run(chunk, action):
@@ -313,7 +305,7 @@
             def _():
                 action(other, chunk_first(other) * GROUP, SIZES[other] * GROUP)
 
-    stages = ((-2, issue_gradients), (2, start_loads), (0, first_phase), (1, second_phase), (2, last_phase), (3, adam), (7, relay), (10, forward))
+    stages = ((-2, issue_gradients), (2, start_loads), (0, first_phase), (1, second_phase), (2, last_phase), (3, adam), (5, relay), (7, forward))
 
     @pl.loop(0, CHUNKS + stages[-1][0])
     def _(t):
@@ -321,14 +313,9 @@
             run(t - lag, action)
 
     drain(acc, d2d_send)
-    for q in range(2):
-        drain(acc.at[0], p1_send.at[q])
-        drain(acc.at[0, pl.ds(0, WINDOW // 2)], p2_send.at[q])
-        drain(wg_ref.at[0, pl.ds(0, WINDOW // 2)], relay_send.at[q])
-        drain(wg_ref.at[0], ag_send.at[q])
-    for q in range(4):
-        drain(wg_ref.at[0], fwd_send.at[q])
-        drain(wg_ref.at[0], fwd_recv.at[q])
+    drain(acc.at[pl.ds(0, 3)], sum_send)
+    drain(wg_ref.at[pl.ds(0, 7)], out_send)
+    drain(wg_ref.at[pl.ds(0, 4)], fwd_recv)
 
     for d in range(1, 8):
         keep = SLICE_ROWS * d - FIRSTS[d] * GROUP
@@ -362,9 +349,8 @@
             pltpu.VMEM((2, 3, CHUNK, LANES), F32),
             pltpu.VMEM((4, SIZES[0] * GROUP, LANES), F32),
             pltpu.VMEM((VEC_ROWS, LANES), F32),
-            dma((4,)), dma((3, 4)), dma, dma((CHUNKS, 4)), dma((2,)), dma((CHUNKS,)), dma((CHUNKS,)), dma((2,)), dma((CHUNKS,)), dma((CHUNKS,)),
-            dma((2, 3)), dma((2,)), dma((CHUNKS,)), dma((CHUNKS,)), dma((2,)), dma((CHUNKS,)), dma((CHUNKS,)),
-            dma((4,)), dma((4,)),
+            dma((2,)), dma((3, 2)), dma, dma((D2D_RING, 2)), dma, dma((RING,)), dma((RING,)), dma((2,)), dma,
+            dma((OUT_RING,)), dma((OUT_RING,)), dma,
         ],
         compiler_params=pltpu.CompilerParams(collective_id=0, has_side_effects=True, vmem_limit_bytes=36 * 1024 * 1024),
     )(*tensors, *state)
@@ -378,15 +364,12 @@
 
 def place_kernel(mv_ref, vv_ref, wv_ref, wg_ref, m_out, v_out, w_out, e_ref, a_ref, f1_ref, f2_ref, b_ref, pair_ref, flat, wide, state_sem, out_sem, pair_sem):
     pair = lax.axis_index('outer') * 2 + lax.axis_index('middle')
-    copies = []
 
     def put(src, dst, sem):
-        copies.append(pltpu.make_async_copy(src, dst, sem))
-        copies[-1].start()
+        pltpu.make_async_copy(src, dst, sem).start()
 
     for q, (src, dst) in enumerate(((mv_ref, m_out), (vv_ref, v_out), (wv_ref, w_out))):
         put(src, dst, state_sem.at[q])
-    count = 0
     for d in range(8):
         low, high = (FIRSTS[d] + 1 if d else 0), FIRSTS[d + 1] + 1
         for q, ref in enumerate((e_ref, a_ref, f1_ref, f2_ref, b_ref)):
@@ -394,11 +377,10 @@
             if begin < end:
                 offset = (begin - BOUNDS[q]) * GROUP
                 size = min((end - begin) * GROUP, ref.shape[0] - offset)
-                put(wg_ref.at[d, pl.ds((begin - window_start(d)) * GROUP, size)], ref.at[pl.ds(offset, size)], out_sem.at[count])
-                count += 1
-
-    def finish(begin, size, sem):
-        put(flat.at[:, pl.ds(begin * LANES, size * LANES)], pair_ref.at[:, pl.ds(begin * LANES, size * LANES)], sem)
+                put(wg_ref.at[d, pl.ds((begin - window_start(d)) * GROUP, size)], ref.at[pl.ds(offset, size)], out_sem)
+
+    def finish(begin, size):
+        put(flat.at[:, pl.ds(begin * LANES, size * LANES)], pair_ref.at[:, pl.ds(begin * LANES, size * LANES)], pair_sem)
 
     def source(group, low, last, starts):
         late = group > last
@@ -412,7 +394,7 @@
             d, row = source(pair * 256 + g, pair, embed_starts[1], embed_starts)
             flat[0:1, pl.ds(pl.multiple_of(g * 4096, 4096), 4096)] = wg_ref[d, pl.ds(row, GROUP)].reshape(1, 4096)
 
-        finish(part * 8192 // PARTS, 8192 // PARTS, pair_sem.at[part])
+        finish(part * 8192 // PARTS, 8192 // PARTS)
 
     for q in (2, 0, 1):
         low = 4 + q
@@ -431,16 +413,19 @@
                     group = wide[turn, g].astype(BF16)
                 flat[0:1, pl.ds(pl.multiple_of((base + layer * 128 + g * GROUP) * LANES, 4096), 4096)] = group.reshape(1, 4096)
 
-        finish(base, 2048, pair_sem.at[PARTS + q])
+        finish(base, 2048)
     lines = []
     for half in range(2):
         tiles = [wg_ref[7, pl.ds(pl.multiple_of(VEC_AT + half * 104 + jnp.minimum(3 * pair + tile, 12) * 8, 8), 8)].astype(F32) for tile in range(5)]
         turned = pltpu.roll(jnp.concatenate(tiles, axis=1), 5 * LANES - 32 * pair, 1)
         lines += [turned[line:line + 1, :416] for line in range(8)]
     flat[0:1, pl.ds(14336 * LANES, 52 * LANES)] = jnp.concatenate(lines, axis=1).astype(BF16)
-    finish(14336, 52, pair_sem.at[PARTS + 3])
-    for copy in copies:
-        copy.wait()
+    finish(14336, 52)
+    for q, (src, dst) in enumerate(((mv_ref, m_out), (vv_ref, v_out), (wv_ref, w_out))):
+        pltpu.make_async_copy(src, dst, state_sem.at[q]).wait()
+    every = wg_ref.at[:, pl.ds(0, SLICE_ROWS)]
+    pltpu.make_async_copy(every, every, out_sem).wait()
+    pltpu.make_async_copy(flat, pair_ref, pair_sem).wait()
 
 
 def place_call(m_new, v_new, w_new, gathered):
@@ -457,7 +442,7 @@
         scratch_shapes=[
             pltpu.VMEM((1, PAIR_SIZE), BF16),
             pltpu.VMEM((2, 4, GROUP, LANES), F32),
-            dma((3,)), dma((12,)), dma((PARTS + 4,)),
+            dma((3,)), dma, dma,
         ],
         compiler_params=pltpu.CompilerParams(vmem_limit_bytes=12 * 1024 * 1024),
     )(*(pltpu.with_memory_space_constraint(x, pltpu.VMEM) for x in (m_new, v_new, w_new, gathered)))

time: 199 us -> 198 us (level)
  Pallas kernels: 199 us -> 197 us
where the time goes in v7:
time: 198 us
  Pallas kernels  197 us (99%)
    pallas_call x1, Pallas kernels, step_call(): pl.pallas_call(step_kernel, name='adam_step', out_shape=(flat, flat, flat...  186 us
    pallas_call x1, Pallas kernels, place_call(): pl.pallas_call(place_kernel, name='place_weights', out_shape=(flat, flat,...  10.8 us

profile of v7, /device:TPU:0, one launch (start us, length us, event | category | flops | bytes accessed | tf_op | source)
XLA Modules:
  0.0 197.9 jit_solution(9042335079178278221)
XLA Ops:
  0.6 186.4 %adam_step.1 = (f32[7194,128]{1,0:T(8,128)S(1)}, f32[7194,128]{1,0:T(8,128)S(1)}, f32[7194,128]{1,0:T(8,128)S(1)}, bf16[8,7232,128]{2,1,0:T(8,128)(2,1)S(1)}) custom-call(f32[32768,128]{1,0:T(8,128)} %bitcast.39, f32[8192,128]{1,0:T(8,128)} %bitcast.40, f32[8192,128]{1,0:T(8,128)} %bitcast.41, f32[8192,128]{1,0:T(8,128)} %bitcast.42, f32[208,128]{1,0:T(8,128)} %bitcast.46, ...), custom_call_target="tpu_custom_call" | custom-call | tf_op jit(solution)/shard_map/adam_step/pallas_call | solution.py:334
  187.1 10.8 %place_weights.1 = (f32[7194,128]{1,0:T(8,128)}, f32[7194,128]{1,0:T(8,128)}, f32[7194,128]{1,0:T(8,128)}, bf16[32768,128]{1,0:T(8,128)(2,1)}, bf16[8192,128]{1,...) custom-call(f32[7194,128]{1,0:T(8,128)S(1)} %get-tuple-element.22.mv, ...), custom_call_target="tpu_custom_call" | custom-call | tf_op jit(solution)/shard_map/place_weights/pallas_call | solution.py:435

commit v8 on v7

--- a/solution.py
+++ b/solution.py
@@ -26,13 +26,14 @@
 CHUNK_GROUPS = 24
 CHUNK = CHUNK_GROUPS * GROUP
 HALF = CHUNK // 2
-LEAD = (4, 12)
+LEAD = (4, 14)
 MAIN = 8
-LAST = (18,)
+LAST = (16,)
 SIZES = LEAD + (CHUNK_GROUPS,) * MAIN + LAST
 CHUNKS = len(SIZES)
 RING = 4
 D2D_RING = 6
+SKEW = 4
 OUT_RING = 5
 WINDOW_GROUPS = sum(SIZES)
 WINDOW = WINDOW_GROUPS * GROUP
@@ -134,59 +135,64 @@
             at = pl.ds(pl.multiple_of(base + off, GROUP), GROUP)
             acc[j, at] = acc[j, at] + term(off)
 
-    def middle(base, size):
-        return base + size // 2 if isinstance(base, int) else pl.multiple_of(base + size // 2, GROUP)
-
-    def first_phase(chunk, base, size):
+    def shifted(base, count):
+        return base + count if isinstance(base, int) else pl.multiple_of(base + count, GROUP)
+
+    def first_phase(chunk, base, size, cuts):
         slot, ring = mod(chunk, 3), mod(chunk, RING)
-        half, second = size // 2, middle(base, size)
-        near = pl.ds(0, half)
+        _, x_cut, y_cut, d_cut = cuts
 
         def ready(j, count):
             arrived = local.at[0, pl.ds(0, count), pl.ds(0, size)]
             drain(arrived, local_sem.at[slot, j])
             drain(arrived, d2d_recv.at[mod(chunk, D2D_RING), j])
 
+        def add(j, first, count):
+            add_rows(j, shifted(base, first), count, lambda off: local[slot, j, pl.ds(first + off, GROUP)])
+
+        def send(j, first, count, dst, place, device):
+            remote(acc.at[j, pl.ds(shifted(base, first), count)], dst.at[ring, place, pl.ds(0, count)], sum_send, p1_recv.at[ring], device)
+
         ready(0, 1)
-        add_rows(3, base, size, lambda off: local[slot, 3, pl.ds(off, GROUP)])
-        remote(acc.at[3, pl.ds(base, half)], p1x.at[ring, 1, near], sum_send, p1_recv.at[ring], x_dev)
-        remote(acc.at[3, pl.ds(second, half)], p1y.at[ring, 1, near], sum_send, p1_recv.at[ring], y_dev)
+        add(3, 0, size)
+        send(3, 0, d_cut, p1x, 1, x_dev)
+        send(3, d_cut, size - d_cut, p1y, 1, y_dev)
         ready(1, 3)
-        add_rows(1, base, half, lambda off: local[slot, 1, pl.ds(off, GROUP)])
-        remote(acc.at[1, pl.ds(base, half)], p1x.at[ring, 0, near], sum_send, p1_recv.at[ring], x_dev)
-        add_rows(2, second, half, lambda off: local[slot, 2, pl.ds(half + off, GROUP)])
-        remote(acc.at[2, pl.ds(second, half)], p1y.at[ring, 0, near], sum_send, p1_recv.at[ring], y_dev)
-        add_rows(1, second, half, lambda off: local[slot, 1, pl.ds(half + off, GROUP)])
-        add_rows(2, base, half, lambda off: local[slot, 2, pl.ds(off, GROUP)])
-        add_rows(0, base, size, lambda off: local[slot, 0, pl.ds(off, GROUP)])
-
-    def second_phase(chunk, base, size):
+        add(1, 0, x_cut)
+        send(1, 0, x_cut, p1x, 0, x_dev)
+        add(2, y_cut, size - y_cut)
+        send(2, y_cut, size - y_cut, p1y, 0, y_dev)
+        add(1, x_cut, size - x_cut)
+        add(2, 0, y_cut)
+        add(0, 0, size)
+
+    def second_phase(chunk, base, size, cuts):
         ring = mod(chunk, RING)
-        half, second = size // 2, middle(base, size)
-        near = pl.ds(0, half)
-        drain(local.at[0, pl.ds(0, 2), pl.ds(0, size)], p1_recv.at[ring])
-        add_rows(2, base, half, lambda off: p1x[ring, 1, pl.ds(off, GROUP)])
-        add_rows(1, second, half, lambda off: p1y[ring, 1, pl.ds(off, GROUP)])
-        remote(acc.at[2, pl.ds(base, half)], p2y.at[ring, near], sum_send, p2_recv.at[ring], y_dev)
-        remote(acc.at[1, pl.ds(second, half)], p2x.at[ring, near], sum_send, p2_recv.at[ring], x_dev)
-        add_rows(0, base, half, lambda off: p1x[ring, 0, pl.ds(off, GROUP)])
-        add_rows(0, second, half, lambda off: p1y[ring, 0, pl.ds(off, GROUP)])
+        cut, x_cut, y_cut, _ = cuts
+        drain(local.at[0, pl.ds(0, 2), pl.ds(0, size + (y_cut - x_cut) // 2)], p1_recv.at[ring])
+        far = shifted(base, x_cut)
+        add_rows(2, base, y_cut, lambda off: p1x[ring, 1, pl.ds(off, GROUP)])
+        add_rows(1, far, size - x_cut, lambda off: p1y[ring, 1, pl.ds(off, GROUP)])
+        remote(acc.at[2, pl.ds(base, y_cut)], p2y.at[ring, pl.ds(0, y_cut)], sum_send, p2_recv.at[ring], y_dev)
+        remote(acc.at[1, pl.ds(far, size - x_cut)], p2x.at[ring, pl.ds(0, size - x_cut)], sum_send, p2_recv.at[ring], x_dev)
+        add_rows(0, base, cut, lambda off: p1x[ring, 0, pl.ds(off, GROUP)])
+        add_rows(0, shifted(base, cut), size - cut, lambda off: p1y[ring, 0, pl.ds(off, GROUP)])
 
     def is_permuted(group):
         return (group >= PERMUTED[0]) & (group < PERMUTED[1])
 
-    def last_phase(chunk, base, size):
+    def last_phase(chunk, base, size, cuts):
         ring = mod(chunk, RING)
-        half = size // 2
+        cut = cuts[0]
         first = start + (base // GROUP if isinstance(base, int) else lax.div(base, GROUP))
         drain(local.at[0, 0, pl.ds(0, size)], p2_recv.at[ring])
-        for part, arrived in enumerate((p2y, p2x)):
-            @pl.loop(0, half // GROUP)
+        for arrived, begin, count in ((p2y, 0, cut), (p2x, cut, size - cut)):
+            @pl.loop(0, count // GROUP)
             def _(r):
                 off = pl.multiple_of(r * GROUP, GROUP)
-                row = pl.multiple_of(base + part * half + off, GROUP)
+                row = pl.multiple_of(base + begin + off, GROUP)
                 total = acc[0, pl.ds(row, GROUP)] + arrived[ring, pl.ds(off, GROUP)]
-                permuted = is_permuted(first + part * (half // GROUP) + r)
+                permuted = is_permuted(first + begin // GROUP + r)
 
                 @pl.when(permuted)
                 def _():
@@ -267,7 +273,7 @@
 
     def relay(chunk, base, size):
         half, turn = size // 2, mod(chunk, OUT_RING)
-        at, head, tail = pl.ds(base, size), pl.ds(base, half), pl.ds(middle(base, size), half)
+        at, head, tail = pl.ds(base, size), pl.ds(base, half), pl.ds(shifted(base, half), half)
         drain(wg_ref.at[pl.ds(0, 2), pl.ds(0, size)], ag_recv.at[turn])
         remote(wg_ref.at[mine[1], head], wg_ref.at[mine[1], head], out_send, relay_recv.at[turn], y_dev)
         remote(wg_ref.at[mine[2], tail], wg_ref.at[mine[2], tail], out_send, relay_recv.at[turn], x_dev)
@@ -293,24 +299,37 @@
         remote(stage.at[j], acc.at[j, pl.ds(0, begin)], d2d_send, d2d_recv.at[0, int(j != 3)], p_dev)
     issue_gradients(1, chunk_first(1) * GROUP, SIZES[1] * GROUP)
 
-    def run(chunk, action):
+    def cut_of(chip, size):
+        return size // 2 + SKEW * GROUP * ((chip == 1) - (chip == 2))
+
+    def run(chunk, action, summing):
         lead = len(LEAD)
+
+        def halves(size):
+            return ((size // 2,) * 4,) if summing else ()
 
         @pl.when((chunk >= lead) & (chunk < lead + MAIN))
         def _():
-            action(chunk, pl.multiple_of(chunk * CHUNK + (sum(LEAD) - lead * CHUNK_GROUPS) * GROUP, GROUP), CHUNK)
+            action(chunk, pl.multiple_of(chunk * CHUNK + (sum(LEAD) - lead * CHUNK_GROUPS) * GROUP, GROUP), CHUNK, *halves(CHUNK))
 
         for other in [*range(lead), *range(lead + MAIN, CHUNKS)]:
             @pl.when(chunk == other)
             def _():
-                action(other, chunk_first(other) * GROUP, SIZES[other] * GROUP)
+                size = SIZES[other] * GROUP
+                if other < CHUNKS - 1 or not halves(size):
+                    action(other, chunk_first(other) * GROUP, size, *halves(size))
+                else:
+                    for chip in range(4):
+                        @pl.when(mine[0] // 2 == chip)
+                        def _():
+                            action(other, chunk_first(other) * GROUP, size, tuple(cut_of(chip ^ j, size) for j in range(4)))
 
     stages = ((-2, issue_gradients), (2, start_loads), (0, first_phase), (1, second_phase), (2, last_phase), (3, adam), (5, relay), (7, forward))
 
     @pl.loop(0, CHUNKS + stages[-1][0])
     def _(t):
         for lag, action in stages:
-            run(t - lag, action)
+            run(t - lag, action, action in (first_phase, second_phase, last_phase))
 
     drain(acc, d2d_send)
     drain(acc.at[pl.ds(0, 3)], sum_send)

time: 198 us -> 197 us (level)
  no operation moved by 1% of the time
where the time goes in v8:
time: 197 us
  Pallas kernels  196 us (99%)
    pallas_call x1, Pallas kernels, step_call(): pl.pallas_call(step_kernel, name='adam_step', out_shape=(flat, flat, flat...  185 us
    pallas_call x1, Pallas kernels, place_call(): pl.pallas_call(place_kernel, name='place_weights', out_shape=(flat, flat,...  10.8 us

profile of v8, /device:TPU:0, one launch (start us, length us, event | category | flops | bytes accessed | tf_op | source)
XLA Modules:
  0.0 196.6 jit_solution(10178420933809906422)
XLA Ops:
  0.6 185.1 %adam_step.1 = (f32[7194,128]{1,0:T(8,128)S(1)}, f32[7194,128]{1,0:T(8,128)S(1)}, f32[7194,128]{1,0:T(8,128)S(1)}, bf16[8,7232,128]{2,1,0:T(8,128)(2,1)S(1)}) custom-call(f32[32768,128]{1,0:T(8,128)} %bitcast.39, f32[8192,128]{1,0:T(8,128)} %bitcast.40, f32[8192,128]{1,0:T(8,128)} %bitcast.41, f32[8192,128]{1,0:T(8,128)} %bitcast.42, f32[208,128]{1,0:T(8,128)} %bitcast.46, ...), custom_call_target="tpu_custom_call" | custom-call | tf_op jit(solution)/shard_map/adam_step/pallas_call | solution.py:353
  185.8 10.8 %place_weights.1 = (f32[7194,128]{1,0:T(8,128)}, f32[7194,128]{1,0:T(8,128)}, f32[7194,128]{1,0:T(8,128)}, bf16[32768,128]{1,0:T(8,128)(2,1)}, bf16[8192,128]{1,...) custom-call(f32[7194,128]{1,0:T(8,128)S(1)} %get-tuple-element.22.mv, ...), custom_call_target="tpu_custom_call" | custom-call | tf_op jit(solution)/shard_map/place_weights/pallas_call | solution.py:454

commit v9 on v8

--- a/solution.py
+++ b/solution.py
@@ -26,14 +26,14 @@
 CHUNK_GROUPS = 24
 CHUNK = CHUNK_GROUPS * GROUP
 HALF = CHUNK // 2
-LEAD = (4, 14)
+LEAD = (4, 12)
 MAIN = 8
-LAST = (16,)
+LAST = (18,)
 SIZES = LEAD + (CHUNK_GROUPS,) * MAIN + LAST
 CHUNKS = len(SIZES)
 RING = 4
 D2D_RING = 6
-SKEW = 4
+SKEW = 3
 OUT_RING = 5
 WINDOW_GROUPS = sum(SIZES)
 WINDOW = WINDOW_GROUPS * GROUP

time: 197 us -> 197 us (level)
  no operation moved by 1% of the time
where the time goes in v9:
time: 197 us
  Pallas kernels  196 us (99%)
    pallas_call x1, Pallas kernels, step_call(): pl.pallas_call(step_kernel, name='adam_step', out_shape=(flat, flat, flat...  185 us
    pallas_call x1, Pallas kernels, place_call(): pl.pallas_call(place_kernel, name='place_weights', out_shape=(flat, flat,...  10.8 us

profile of v9, /device:TPU:0, one launch (start us, length us, event | category | flops | bytes accessed | tf_op | source)
XLA Modules:
  0.0 196.9 jit_solution(6364100500975529392)
XLA Ops:
  0.6 185.4 %adam_step.1 = (f32[7194,128]{1,0:T(8,128)S(1)}, f32[7194,128]{1,0:T(8,128)S(1)}, f32[7194,128]{1,0:T(8,128)S(1)}, bf16[8,7232,128]{2,1,0:T(8,128)(2,1)S(1)}) custom-call(f32[32768,128]{1,0:T(8,128)} %bitcast.39, f32[8192,128]{1,0:T(8,128)} %bitcast.40, f32[8192,128]{1,0:T(8,128)} %bitcast.41, f32[8192,128]{1,0:T(8,128)} %bitcast.42, f32[208,128]{1,0:T(8,128)} %bitcast.46, ...), custom_call_target="tpu_custom_call" | custom-call | tf_op jit(solution)/shard_map/adam_step/pallas_call | solution.py:353
  186.0 10.8 %place_weights.1 = (f32[7194,128]{1,0:T(8,128)}, f32[7194,128]{1,0:T(8,128)}, f32[7194,128]{1,0:T(8,128)}, bf16[32768,128]{1,0:T(8,128)(2,1)}, bf16[8192,128]{1,...) custom-call(f32[7194,128]{1,0:T(8,128)S(1)} %get-tuple-element.22.mv, ...), custom_call_target="tpu_custom_call" | custom-call | tf_op jit(solution)/shard_map/place_weights/pallas_call | solution.py:454

commit v10 on v9

--- a/solution.py
+++ b/solution.py
@@ -23,12 +23,12 @@
 GROUP = 32
 ROWS = 7366656 // LANES
 SLICE_ROWS = ROWS // 8
-CHUNK_GROUPS = 24
+CHUNK_GROUPS = 20
 CHUNK = CHUNK_GROUPS * GROUP
 HALF = CHUNK // 2
 LEAD = (4, 12)
-MAIN = 8
-LAST = (18,)
+MAIN = 10
+LAST = (10,)
 SIZES = LEAD + (CHUNK_GROUPS,) * MAIN + LAST
 CHUNKS = len(SIZES)
 RING = 4

time: 197 us -> 197 us (level)
  no operation moved by 1% of the time
where the time goes in v10:
time: 197 us
  Pallas kernels  196 us (99%)
    pallas_call x1, Pallas kernels, step_call(): pl.pallas_call(step_kernel, name='adam_step', out_shape=(flat, flat, flat...  186 us
    pallas_call x1, Pallas kernels, place_call(): pl.pallas_call(place_kernel, name='place_weights', out_shape=(flat, flat,...  10.8 us

profile of v10, /device:TPU:0, one launch (start us, length us, event | category | flops | bytes accessed | tf_op | source)
XLA Modules:
  0.0 197.0 jit_solution(7205924856624765678)
XLA Ops:
  0.6 185.6 %adam_step.1 = (f32[7194,128]{1,0:T(8,128)S(1)}, f32[7194,128]{1,0:T(8,128)S(1)}, f32[7194,128]{1,0:T(8,128)S(1)}, bf16[8,7232,128]{2,1,0:T(8,128)(2,1)S(1)}) custom-call(f32[32768,128]{1,0:T(8,128)} %bitcast.39, f32[8192,128]{1,0:T(8,128)} %bitcast.40, f32[8192,128]{1,0:T(8,128)} %bitcast.41, f32[8192,128]{1,0:T(8,128)} %bitcast.42, f32[208,128]{1,0:T(8,128)} %bitcast.46, ...), custom_call_target="tpu_custom_call" | custom-call | tf_op jit(solution)/shard_map/adam_step/pallas_call | solution.py:353
  186.2 10.8 %place_weights.1 = (f32[7194,128]{1,0:T(8,128)}, f32[7194,128]{1,0:T(8,128)}, f32[7194,128]{1,0:T(8,128)}, bf16[32768,128]{1,0:T(8,128)(2,1)}, bf16[8192,128]{1,...) custom-call(f32[7194,128]{1,0:T(8,128)S(1)} %get-tuple-element.22.mv, ...), custom_call_target="tpu_custom_call" | custom-call | tf_op jit(solution)/shard_map/place_weights/pallas_call | solution.py:454

commit v11 on v9

--- a/solution.py
+++ b/solution.py
@@ -26,9 +26,9 @@
 CHUNK_GROUPS = 24
 CHUNK = CHUNK_GROUPS * GROUP
 HALF = CHUNK // 2
-LEAD = (4, 12)
+LEAD = (4, 16)
 MAIN = 8
-LAST = (18,)
+LAST = (14,)
 SIZES = LEAD + (CHUNK_GROUPS,) * MAIN + LAST
 CHUNKS = len(SIZES)
 RING = 4

time: 197 us -> 197 us (level)
  no operation moved by 1% of the time
where the time goes in v11:
time: 197 us
  Pallas kernels  196 us (99%)
    pallas_call x1, Pallas kernels, step_call(): pl.pallas_call(step_kernel, name='adam_step', out_shape=(flat, flat, flat...  185 us
    pallas_call x1, Pallas kernels, place_call(): pl.pallas_call(place_kernel, name='place_weights', out_shape=(flat, flat,...  10.8 us

profile of v11, /device:TPU:0, one launch (start us, length us, event | category | flops | bytes accessed | tf_op | source)
XLA Modules:
  0.0 196.8 jit_solution(5850867336942250223)
XLA Ops:
  0.6 185.3 %adam_step.1 = (f32[7194,128]{1,0:T(8,128)S(1)}, f32[7194,128]{1,0:T(8,128)S(1)}, f32[7194,128]{1,0:T(8,128)S(1)}, bf16[8,7232,128]{2,1,0:T(8,128)(2,1)S(1)}) custom-call(f32[32768,128]{1,0:T(8,128)} %bitcast.39, f32[8192,128]{1,0:T(8,128)} %bitcast.40, f32[8192,128]{1,0:T(8,128)} %bitcast.41, f32[8192,128]{1,0:T(8,128)} %bitcast.42, f32[208,128]{1,0:T(8,128)} %bitcast.46, ...), custom_call_target="tpu_custom_call" | custom-call | tf_op jit(solution)/shard_map/adam_step/pallas_call | solution.py:353
  186.0 10.8 %place_weights.1 = (f32[7194,128]{1,0:T(8,128)}, f32[7194,128]{1,0:T(8,128)}, f32[7194,128]{1,0:T(8,128)}, bf16[32768,128]{1,0:T(8,128)(2,1)}, bf16[8192,128]{1,...) custom-call(f32[7194,128]{1,0:T(8,128)S(1)} %get-tuple-element.22.mv, ...), custom_call_target="tpu_custom_call" | custom-call | tf_op jit(solution)/shard_map/place_weights/pallas_call | solution.py:454
